TPU v7x, 32 devices: a whole 2x2x4 slice. The times are simulated.
32 devices in a mesh: gx: 2 (over x), gy: 4 (over z), band: 4 (over y, core).
Axes of the slice: x: 2, y: 2, z: 4, core: 2. Of those that a mesh axis runs over, the one named last changes fastest.
Arguments:
- orbitals: float32 [2, 16, 16, 48, 128], P(None, 'band', 'gx', 'gy'), may hold values from -3 to 3
- external: float32 [16, 48, 128], P('gx', 'gy'), may hold values from 2 to 6
Outputs:
- orbitals_next: float32 [2, 16, 16, 48, 128], P(None, 'band', 'gx', 'gy')
- potential_next: float32 [16, 48, 128], P('gx', 'gy')
All inputs are finite; a program needn't handle non-finite values.
Results may differ from a plain program's by a relative error of at most 0.00002.
Values sent between devices are 32-bit elements; how exact they have to be, the bound alone decides.
No kernel may reach another device: no remote copies, remote signals or barrier semaphores. Data moves between devices by JAX's collectives and lax.ppermute only.
A program may use at most 64 MiB of HBM per device.

v0:
```python
import functools

import jax
import jax.numpy as jnp
from jax import lax
from jax.experimental import pallas as pl
from jax.experimental.pallas import tpu as pltpu
from jax.sharding import PartitionSpec as P


step_length = 0.15
exchange_coef = 0.7386
ORDER = 4
WIDE = 2 * ORDER
AXES = ("gx", "gy", "band")
LANES = 128


def corner_depth(d):
    return 2 * (ORDER - (d + 1) // 2)


def partner(kind, index, count):
    other = index ^ 1 if kind == 0 else ((index + 1) ^ 1) - 1
    return other if 0 <= other < count else None


def divisor(count, limit):
    return max(n for n in range(1, limit + 1) if count % n == 0)


class Plan:
    def __init__(self, mesh, shape):
        self.gx, self.gy, self.groups = (mesh.shape[a] for a in AXES)
        self.parts, self.bands, self.cols, self.rows, self.depth = shape
        self.fields = self.parts * self.bands
        self.cells = self.rows * self.cols
        self.xs = tuple(k for k in (0, 1) if k < self.gx - 1)
        self.ys = tuple(k for k in (0, 1) if k < self.gy - 1)
        self.ext_rows = self.rows + 2 * WIDE
        self.ext_cols = self.cols + 2 * WIDE
        self.corner = sum(corner_depth(d) for d in range(1, WIDE - 1))
        self.v_cols = WIDE // 2
        self.edge_cells = len(self.xs) * self.v_cols + WIDE
        self.wide_cells = WIDE * self.rows

    def pairs(self, kx=None, ky=None, flip=0):
        index = lambda i, j, b: (i * self.gy + j) * self.groups + b
        out = []
        for i in range(self.gx):
            for j in range(self.gy):
                for b in range(self.groups):
                    i2 = i if kx is None else partner(kx, i, self.gx)
                    j2 = j if ky is None else partner(ky, j, self.gy)
                    to = (i, j, b ^ 1) if i2 is None or j2 is None else (i2, j2, b ^ flip)
                    out.append((index(i, j, b), index(*to)))
        return out

    def swap(self, value, **kinds):
        return lax.ppermute(value, AXES, self.pairs(**kinds))

    def above(self, axis, kind):
        return lax.rem(lax.axis_index(axis), 2) == kind

    def near(self, hi, size, extent):
        return 0 if size == extent else jnp.where(hi, extent - size, 0)

    def beyond(self, hi, size, extent):
        return jnp.where(hi, WIDE + extent, WIDE - size)

    def at_partner(self, hi, size, extent):
        return 0 if size == extent else jnp.where(hi, 0, extent - size)

    def span(self, reach):
        if len(self.xs) == 2:
            return WIDE - reach, self.rows + 2 * reach
        if not self.xs:
            return WIDE, self.rows
        return jnp.where(self.above("gx", 0), WIDE, WIDE - reach), self.rows + reach


def pack(plan, fields_ref, out_refs):
    out_refs = list(out_refs)
    for ky in plan.ys:
        base, out = plan.near(plan.above("gy", ky), WIDE, plan.cols), out_refs.pop(0)
        for c in range(WIDE):
            out[pl.ds(c * plan.rows, plan.rows)] = fields_ref[pl.ds((base + c) * plan.rows, plan.rows)]
    for ky in plan.ys:
        hi = plan.above("gy", ky)
        for kx in plan.xs:
            x_hi, out, at = plan.above("gx", kx), out_refs.pop(0), 0
            for d in range(1, WIDE - 1):
                size = corner_depth(d)
                col = jnp.where(hi, plan.cols - d, d - 1)
                out[at : at + size] = fields_ref[pl.ds(col * plan.rows + plan.near(x_hi, size, plan.rows), size)]
                at += size


def enter_kernel(plan, orb_ref, fields_ref, dens_ref, *rest):
    *packed, flat = rest
    f, rows = plan.fields, plan.rows
    for c in range(plan.cols):
        total = None
        for p in range(plan.parts):
            for b in range(plan.bands):
                v = orb_ref[p, b, c]
                flat[pl.ds(c * rows * f + p * plan.bands + b, rows, stride=f), :] = v
                total = v * v if total is None else total + v * v
        dens_ref[c] = total
        for r in range(c * rows, (c + 1) * rows):
            fields_ref[r] = flat[r * f : (r + 1) * f, :]
    pack(plan, fields_ref, packed)


def cube_root(value):
    root = jnp.exp(jnp.log(value) * (1.0 / 3.0))
    cubed = root * root * root
    better = root * (cubed + 2.0 * value) / (2.0 * cubed + value)
    return jnp.where(root > 1e-10, better, root)


def potential_kernel(ext_ref, *refs):
    *parts, out = refs
    total = parts[0][...]
    for q in parts[1:]:
        total = total + q[...]
    out[...] = ext_ref[...] - exchange_coef * cube_root(total)


def edge_kernel(plan, v_here, *refs):
    nx = len(plan.xs)
    v_there, out = refs[:nx], refs[nx:]
    for ky, o in zip(plan.ys, out):
        hi = plan.above("gy", ky)
        o[0:WIDE] = v_here[pl.ds(plan.near(hi, WIDE, plan.cols), WIDE)]
        for n in range(nx):
            at = WIDE + n * plan.v_cols
            o[at : at + plan.v_cols] = v_there[n][pl.ds(plan.near(hi, plan.v_cols, plan.cols), plan.v_cols)]


def evolve_kernel(plan, final, *refs):
    nx, ny = len(plan.xs), len(plan.ys)
    refs = list(refs)
    take = lambda n: [refs.pop(0) for _ in range(n)]
    (own,) = take(1)
    far, big = take(nx), take(ny)
    corners = [take(nx) for _ in range(ny)]
    (v_here,) = take(1)
    v_there, edge = take(nx), take(ny)
    if final:
        orb_ref, v_out = take(2)
    else:
        (half_ref, dens_ref) = take(2)
        packed = take(ny + nx * ny)
    levels = take(ORDER)
    (pot,) = take(1)
    if final:
        (flat,) = take(1)
    rows, cols, f = plan.rows, plan.cols, plan.fields
    long = plan.ext_rows
    i, j = lax.axis_index("gx"), lax.axis_index("gy")
    h0 = levels[0]

    def put_potential(first, v, count):
        scaled = 24.0 * v + 90.0
        for t in range(count):
            pot[first + t] = jnp.broadcast_to(scaled[t : t + 1, :], (f, LANES))

    for c in range(cols):
        at = (WIDE + c) * long + WIDE
        h0[at : at + rows] = own[c * rows : (c + 1) * rows]
        put_potential(at, v_here[c], rows)
    for n, kx in enumerate(plan.xs):
        x_hi = plan.above("gx", kx)
        row, src = plan.beyond(x_hi, WIDE, rows), plan.at_partner(x_hi, WIDE, rows)
        for c in range(cols):
            at = (WIDE + c) * long + row
            h0[pl.ds(at, WIDE)] = far[n][pl.ds(c * rows + src, WIDE)]
            put_potential(at, v_there[n][c, pl.ds(src, WIDE), :], WIDE)
    for n, ky in enumerate(plan.ys):
        hi = plan.above("gy", ky)
        base = plan.beyond(hi, WIDE, cols)
        for c in range(WIDE):
            at = (base + c) * long + WIDE
            h0[pl.ds(at, rows)] = big[n][pl.ds(c * rows, rows)]
            put_potential(at, edge[n][c], rows)
        for n_x, kx in enumerate(plan.xs):
            at = WIDE + n_x * plan.v_cols
            x_hi = plan.above("gx", kx)
            row, src = plan.beyond(x_hi, WIDE, rows), plan.at_partner(x_hi, WIDE, rows)
            first = plan.beyond(hi, plan.v_cols, cols)
            for c in range(plan.v_cols):
                put_potential((first + c) * long + row, edge[n][at + c, pl.ds(src, WIDE), :], WIDE)
            at = 0
            for d in range(1, WIDE - 1):
                size = corner_depth(d)
                col = jnp.where(hi, WIDE + cols + d - 1, WIDE - d)
                h0[pl.ds(col * long + plan.beyond(x_hi, size, rows), size)] = corners[n][n_x][at : at + size]
                at += size

    def clear_outside(h):
        for outside, col in ((j == 0, WIDE - 2), (j == plan.gy - 1, WIDE + cols)):

            @pl.when(outside)
            def _(col=col):
                for c in (col, col + 1):
                    h[c * long : (c + 1) * long] = jnp.zeros((long, f, LANES), jnp.float32)

        for outside, row in ((i == 0, WIDE - 2), (i == plan.gx - 1, WIDE + rows)):

            @pl.when(outside)
            def _(row=row):
                for c in range(plan.ext_cols):
                    h[c * long + row : c * long + row + 2] = jnp.zeros((2, f, LANES), jnp.float32)

    lane = lax.broadcasted_iota(jnp.int32, (f, LANES), 1)
    shifts = ((1, lane >= 1), (LANES - 1, lane < LANES - 1), (2, lane >= 2), (LANES - 2, lane < LANES - 2))

    def image(h, first, count, use):
        line = [h[first + t] for t in range(-2, 2)]
        for t in range(count):
            at = first + t
            line.append(h[at + 2])
            v = line[2]
            z = [jnp.where(keep, pltpu.roll(v, s, 1), 0.0) for s, keep in shifts]
            near = (line[1] + line[3]) + (h[at - long] + h[at + long]) + (z[0] + z[1])
            outer = (line[0] + line[4]) + (h[at - 2 * long] + h[at + 2 * long]) + (z[2] + z[3])
            use(at, t, (outer - 16.0 * near) + pot[at] * v)
            line.pop(0)

    clear_outside(h0)
    for k in range(1, ORDER):
        source, target = levels[k - 1], levels[k]

        def column(col, reach, source=source, target=target):
            row, count = plan.span(reach)

            def store(at, t, value):
                target[at] = value

            image(source, col * long + row, count, store)

        reach = 2 * (ORDER - k)

        @pl.loop(0, cols, unroll=divisor(cols, 6))
        def _(c, reach=reach, column=column):
            column(WIDE + c, reach)

        for m in range(1, ORDER - k + 1):
            if plan.ys:

                @pl.loop(0, 4, unroll=4)
                def _(t, m=m, reach=reach, column=column):
                    col = jnp.where(t < 2, WIDE - 2 * m, WIDE + cols + 2 * m - 4)
                    column(col + t, reach - 2 * m)

        clear_outside(target)

    sign = jnp.where(lax.broadcasted_iota(jnp.int32, (f, LANES), 0) < plan.bands, 1.0, -1.0)

    def total(s, g):
        a = [(s / 24.0) ** k for k in range(ORDER + 1)]
        even = g[0] - (a[2] / 2) * g[2] + (a[4] / 24) * g[4]
        odd = a[1] * g[1] - (a[3] / 6) * g[3]
        return even + sign * pltpu.roll(odd, plan.bands, 0)

    @pl.loop(0, cols, unroll=divisor(cols, 6))
    def _(c):
        def finish(at, t, value):
            g = [h[at] for h in levels] + [value]
            half = total(step_length / 2, g)
            cell = c * rows + t
            if final:
                flat[pl.ds(pl.multiple_of(cell * f, f), f), :] = half
            else:
                half_ref[cell] = half
                full = total(step_length, g)
                dens_ref[c, t : t + 1, :] = jnp.sum(full * full, axis=0, keepdims=True)

        image(levels[-1], (WIDE + c) * long + WIDE, rows, finish)

    if final:
        v_out[...] = v_here[...]
        for c in range(cols):
            for p in range(plan.parts):
                for b in range(plan.bands):
                    first = c * rows * f + p * plan.bands + b
                    orb_ref[p, b, c] = flat[pl.ds(first, rows, stride=f), :]
    else:
        pack(plan, half_ref, packed)


def call(kernel, outs, scratch=(), limit=8):
    spec = pl.BlockSpec(memory_space=pltpu.VMEM)
    return lambda *args: pl.pallas_call(
        kernel,
        out_shape=[jax.ShapeDtypeStruct(s, jnp.float32) for s in outs],
        in_specs=[spec] * len(args),
        out_specs=[spec] * len(outs),
        scratch_shapes=list(scratch),
        compiler_params=pltpu.CompilerParams(vmem_limit_bytes=limit << 20),
    )(*args)


def solution(mesh):
    def body(orbitals, external):
        orbitals, external = jnp.swapaxes(orbitals, 2, 3), jnp.swapaxes(external, 0, 1)
        plan = Plan(mesh, orbitals.shape)
        f, cells = plan.fields, plan.cells
        field_shape, plane = (cells, f, LANES), (plan.cols, plan.rows, LANES)
        wide = (plan.wide_cells, f, LANES)
        nx, ny = len(plan.xs), len(plan.ys)
        packed = [wide] * ny + [(plan.corner, f, LANES)] * (nx * ny)

        fields, dens, *out = call(
            functools.partial(enter_kernel, plan),
            [field_shape, plane] + packed,
            [pltpu.VMEM((cells * f, LANES), jnp.float32)],
        )(orbitals)

        def gather(fields, dens, out):
            def swap(value, **kinds):
                return plan.swap(value, **kinds)

            far = [swap(fields, kx=k) for k in plan.xs]
            big = [swap(v, ky=k) for k, v in zip(plan.ys, out)]
            both = [(ky, kx) for ky in plan.ys for kx in plan.xs]
            corners = [swap(v, kx=kx, ky=ky) for (ky, kx), v in zip(both, out[ny:])]
            dens = dens + swap(dens, flip=1)
            more = [swap(dens, flip=b) for b in range(2, plan.groups, 2)]
            (v_here,) = call(potential_kernel, [plane])(external, dens, *more)
            v_there = [swap(v_here, kx=k) for k in plan.xs]
            edge = call(
                functools.partial(edge_kernel, plan), [(plan.edge_cells, plan.rows, LANES)] * ny
            )(v_here, *v_there)
            edge = [swap(v, ky=k) for k, v in zip(plan.ys, edge)]
            return [*far, *big, *corners, v_here, *v_there, *edge]

        extended = pltpu.VMEM((plan.ext_rows * plan.ext_cols, f, LANES), jnp.float32)
        scratch = [extended] * (ORDER + 1)
        arrived = gather(fields, dens, out)
        half, dens, *out = call(
            functools.partial(evolve_kernel, plan, False), [field_shape, plane] + packed, scratch, limit=24
        )(fields, *arrived)
        arrived = gather(half, dens, out)
        result, potential = call(
            functools.partial(evolve_kernel, plan, True),
            [orbitals.shape, plane],
            scratch + [pltpu.VMEM((cells * f, LANES), jnp.float32)],
            limit=24,
        )(half, *arrived)
        return jnp.swapaxes(result, 2, 3), jnp.swapaxes(potential, 0, 1)

    in_specs = (P(None, "band", "gx", "gy", None), P("gx", "gy", None))
    out_specs = (P(None, "band", "gx", "gy", None), P("gx", "gy", None))
    return jax.shard_map(body, mesh=mesh, in_specs=in_specs, out_specs=out_specs, check_vma=False)
```

profile of v0, /device:TPU:12, one launch (start us, length us, event | category | flops | bytes accessed | tf_op | source)
XLA Modules:
  0.0 57.0 jit_solution(12829550302614711590)
XLA Ops:
  0.6 1.0 %copy-done = f32[2,4,8,12,128]{4,2,3,1,0:T(8,128)S(1)} copy-done((f32[2,4,8,12,128]{4,2,3,1,0:T(8,128)S(1)}, f32[2,4,8,12,128]{4,2,3,1,0:T(8,128)}, u32[]{:S(2)}) %copy-start) | copy-done | bytes 393240
  1.8 1.6 %collective-permute-start = (f32[96,8,128]{2,1,0:T(8,128)S(1)}, f32[96,8,128]{2,1,0:T(8,128)S(1)}, u32[]{:S(2)}, u32[]{:S(2)}) collective-permute-start(f32[96,8,128]{2,1,0:T(8,128)S(1)} %get-tuple-element.20.refs_0_), channel_id=1, source_target_pairs={{0,16},{1,17},{2,18},{3,19},{4,20},{5,21},{6,22},{7,23},{8,24},{9,... | collective-permute-start | bytes 1179656 | tf_op jit(solution)/shard_map/ppermute | solution.py:60
  3.3 0.4 collective-permute-start.1
  3.8 2.7 %collective-permute-start.2 = (f32[64,8,128]{2,1,0:T(8,128)S(1)}, f32[64,8,128]{2,1,0:T(8,128)S(1)}, u32[]{:S(2)}, u32[]{:S(2)}) collective-permute-start(f32[64,8,128]{2,1,0:T(8,128)S(1)} %get-tuple-element.22), channel_id=1, source_target_pairs={{0,1},{1,0},{2,3},{3,2},{4,8},{5,9},{6,10},{7,11},{8,4},{9,5},{10,... | collective-permute-start | bytes 786440 | tf_op jit(solution)/shard_map/ppermute | solution.py:60
  6.5 0.6 %collective-permute-start.6 = (f32[12,8,128]{2,1,0:T(8,128)S(1)}, f32[12,8,128]{2,1,0:T(8,128)S(1)}, u32[]{:S(2)}, u32[]{:S(2)}) collective-permute-start(f32[12,8,128]{2,1,0:T(8,128)S(1)} %add.6.refs_0_), channel_id=1, source_target_pairs={{0,2},{1,3},{2,0},{3,1},{4,6},{5,7},{6,4},{7,5},{8,10},{9,11},{10,... | collective-permute-start | bytes 147464 | tf_op jit(solution)/shard_map/ppermute | solution.py:60
  7.1 3.6 %collective-permute-done.6.refs_1_ = f32[12,8,128]{2,1,0:T(8,128)S(1)} collective-permute-done((f32[12,8,128]{2,1,0:T(8,128)S(1)}, f32[12,8,128]{2,1,0:T(8,128)S(1)}, u32[]{:S(2)}, u32[]{:S(2)}) %collective-permute-start.6) | collective-permute-done | bytes 49184 | tf_op jit(solution)/shard_map/ppermute | solution.py:60
  10.7 0.6 %collective-permute-start.7 = (f32[12,8,128]{2,1,0:T(8,128)S(1)}, f32[12,8,128]{2,1,0:T(8,128)S(1)}, u32[]{:S(2)}, u32[]{:S(2)}) collective-permute-start(f32[12,8,128]{2,1,0:T(8,128)S(1)} %shard_map.42.v_here.refs_6_), channel_id=1, source_target_pairs={{0,16},{1,17},{2,18},{3,19},{4,20},{5,21},{6,22},{7,23},{8,24},{9,... | collective-permute-start | bytes 147464 | tf_op jit(solution)/shard_map/ppermute | solution.py:60
  11.3 3.9 %collective-permute-done.7.refs_0_.refs_7_ = f32[12,8,128]{2,1,0:T(8,128)S(1)} collective-permute-done((f32[12,8,128]{2,1,0:T(8,128)S(1)}, f32[12,8,128]{2,1,0:T(8,128)S(1)}, u32[]{:S(2)}, u32[]{:S(2)}) %collective-permute-start.7) | collective-permute-done | bytes 49184 | tf_op jit(solution)/shard_map/ppermute | solution.py:60
  15.2 3.2 %collective-permute-start.4 = (f32[24,8,128]{2,1,0:T(8,128)S(1)}, f32[24,8,128]{2,1,0:T(8,128)S(1)}, u32[]{:S(2)}, u32[]{:S(2)}) collective-permute-start(f32[24,8,128]{2,1,0:T(8,128)S(1)} %get-tuple-element.24), channel_id=1, source_target_pairs={{0,1},{1,0},{2,3},{3,2},{4,24},{5,25},{6,26},{7,27},{8,20},{9,21},... | collective-permute-start | bytes 294920 | tf_op jit(solution)/shard_map/ppermute | solution.py:60
  18.4 2.6 %collective-permute-done.4.refs_5_ = f32[24,8,128]{2,1,0:T(8,128)S(1)} collective-permute-done((f32[24,8,128]{2,1,0:T(8,128)S(1)}, f32[24,8,128]{2,1,0:T(8,128)S(1)}, u32[]{:S(2)}, u32[]{:S(2)}) %collective-permute-start.4) | collective-permute-done | bytes 98336 | tf_op jit(solution)/shard_map/ppermute | solution.py:60
  21.0 1.9 %collective-permute-start.9 = (f32[12,8,128]{2,1,0:T(8,128)S(1)}, f32[12,8,128]{2,1,0:T(8,128)S(1)}, u32[]{:S(2)}, u32[]{:S(2)}) collective-permute-start(f32[12,8,128]{2,1,0:T(8,128)S(1)} %get-tuple-element.27), channel_id=1, source_target_pairs={{0,1},{1,0},{2,3},{3,2},{4,8},{5,9},{6,10},{7,11},{8,4},{9,5},{10,... | collective-permute-start | bytes 147464 | tf_op jit(solution)/shard_map/ppermute | solution.py:60
  22.9 2.2 %collective-permute-done.9.refs_9_ = f32[12,8,128]{2,1,0:T(8,128)S(1)} collective-permute-done((f32[12,8,128]{2,1,0:T(8,128)S(1)}, f32[12,8,128]{2,1,0:T(8,128)S(1)}, u32[]{:S(2)}, u32[]{:S(2)}) %collective-permute-start.9) | collective-permute-done | bytes 49184 | tf_op jit(solution)/shard_map/ppermute | solution.py:60
  25.1 4.4 %shard_map.44 = (f32[96,8,128]{2,1,0:T(8,128)S(1)}, f32[12,8,128]{2,1,0:T(8,128)S(1)}, f32[64,8,128]{2,1,0:T(8,128)S(1)}, f32[64,8,128]{2,1,0:T(8,128)S(1)}, f32...) custom-call(f32[96,8,128]{2,1,0:T(8,128)S(1)} %get-tuple-element.20.refs_0_, ...), custom_call_target="tpu_custom_call" | custom-call | tf_op jit(solution)/shard_map/pallas_call | solution.py:295
  29.5 2.0 %collective-permute-start.10 = (f32[96,8,128]{2,1,0:T(8,128)S(1)}, f32[96,8,128]{2,1,0:T(8,128)S(1)}, u32[]{:S(2)}, u32[]{:S(2)}) collective-permute-start(f32[96,8,128]{2,1,0:T(8,128)S(1)} %get-tuple-element.28.refs_0_), channel_id=1, source_target_pairs={{0,16},{1,17},{2,18},{3,19},{4,20},{5,21},{6,22},{7,23},{8,24},{9,... | collective-permute-start | bytes 1179656 | tf_op jit(solution)/shard_map/ppermute | solution.py:60
  31.5 2.0 %collective-permute-start.12 = (f32[64,8,128]{2,1,0:T(8,128)S(1)}, f32[64,8,128]{2,1,0:T(8,128)S(1)}, u32[]{:S(2)}, u32[]{:S(2)}) collective-permute-start(f32[64,8,128]{2,1,0:T(8,128)S(1)} %get-tuple-element.30), channel_id=1, source_target_pairs={{0,1},{1,0},{2,3},{3,2},{4,8},{5,9},{6,10},{7,11},{8,4},{9,5},{10,... | collective-permute-start | bytes 786440 | tf_op jit(solution)/shard_map/ppermute | solution.py:60
  33.5 0.6 %collective-permute-start.16 = (f32[12,8,128]{2,1,0:T(8,128)S(1)}, f32[12,8,128]{2,1,0:T(8,128)S(1)}, u32[]{:S(2)}, u32[]{:S(2)}) collective-permute-start(f32[12,8,128]{2,1,0:T(8,128)S(1)} %add.7.refs_0_), channel_id=1, source_target_pairs={{0,2},{1,3},{2,0},{3,1},{4,6},{5,7},{6,4},{7,5},{8,10},{9,11},{10,... | collective-permute-start | bytes 147464 | tf_op jit(solution)/shard_map/ppermute | solution.py:60
  34.1 3.6 %collective-permute-done.16.refs_1_ = f32[12,8,128]{2,1,0:T(8,128)S(1)} collective-permute-done((f32[12,8,128]{2,1,0:T(8,128)S(1)}, f32[12,8,128]{2,1,0:T(8,128)S(1)}, u32[]{:S(2)}, u32[]{:S(2)}) %collective-permute-start.16) | collective-permute-done | bytes 49184 | tf_op jit(solution)/shard_map/ppermute | solution.py:60
  38.0 1.5 %collective-permute-start.13 = (f32[24,8,128]{2,1,0:T(8,128)S(1)}, f32[24,8,128]{2,1,0:T(8,128)S(1)}, u32[]{:S(2)}, u32[]{:S(2)}) collective-permute-start(f32[24,8,128]{2,1,0:T(8,128)S(1)} %get-tuple-element.31), channel_id=1, source_target_pairs={{0,20},{1,21},{2,22},{3,23},{4,16},{5,17},{6,18},{7,19},{8,28},{9,... | collective-permute-start | bytes 294920 | tf_op jit(solution)/shard_map/ppermute | solution.py:60
  39.5 2.8 %collective-permute-done.17.refs_0_.refs_7_ = f32[12,8,128]{2,1,0:T(8,128)S(1)} collective-permute-done((f32[12,8,128]{2,1,0:T(8,128)S(1)}, f32[12,8,128]{2,1,0:T(8,128)S(1)}, u32[]{:S(2)}, u32[]{:S(2)}) %collective-permute-start.17) | collective-permute-done | bytes 49184 | tf_op jit(solution)/shard_map/ppermute | solution.py:60
  42.6 0.9 %collective-permute-done.13.refs_4_ = f32[24,8,128]{2,1,0:T(8,128)S(1)} collective-permute-done((f32[24,8,128]{2,1,0:T(8,128)S(1)}, f32[24,8,128]{2,1,0:T(8,128)S(1)}, u32[]{:S(2)}, u32[]{:S(2)}) %collective-permute-start.13) | collective-permute-done | bytes 98336 | tf_op jit(solution)/shard_map/ppermute | solution.py:60
  43.9 4.0 %collective-permute-done.14.refs_5_ = f32[24,8,128]{2,1,0:T(8,128)S(1)} collective-permute-done((f32[24,8,128]{2,1,0:T(8,128)S(1)}, f32[24,8,128]{2,1,0:T(8,128)S(1)}, u32[]{:S(2)}, u32[]{:S(2)}) %collective-permute-start.14) | collective-permute-done | bytes 98336 | tf_op jit(solution)/shard_map/ppermute | solution.py:60
  47.8 1.1 %collective-permute-start.19 = (f32[12,8,128]{2,1,0:T(8,128)S(1)}, f32[12,8,128]{2,1,0:T(8,128)S(1)}, u32[]{:S(2)}, u32[]{:S(2)}) collective-permute-start(f32[12,8,128]{2,1,0:T(8,128)S(1)} %get-tuple-element.35), channel_id=1, source_target_pairs={{0,1},{1,0},{2,3},{3,2},{4,8},{5,9},{6,10},{7,11},{8,4},{9,5},{10,... | collective-permute-start | bytes 147464 | tf_op jit(solution)/shard_map/ppermute | solution.py:60
  48.9 3.0 %collective-permute-done.19.refs_9_ = f32[12,8,128]{2,1,0:T(8,128)S(1)} collective-permute-done((f32[12,8,128]{2,1,0:T(8,128)S(1)}, f32[12,8,128]{2,1,0:T(8,128)S(1)}, u32[]{:S(2)}, u32[]{:S(2)}) %collective-permute-start.19) | collective-permute-done | bytes 49184 | tf_op jit(solution)/shard_map/ppermute | solution.py:60
  51.9 5.1 %shard_map.47 = (f32[2,4,12,8,128]{4,3,2,1,0:T(8,128)}, f32[12,8,128]{2,1,0:T(8,128)}) custom-call(f32[96,8,128]{2,1,0:T(8,128)S(1)} %get-tuple-element.28.refs_0_, f32[96,8,128]{2,1,0:T(8,128)S(1)} %collective-permute-done.10.refs_1_, f32[64,8,128]{2,1,0:T(8,128)S(1)} %collective-permute-done.11.refs_2_, f32[64,8,128]{2,1,0:T(8,128)S(1)} %collective-permute-done.12.refs_3_, ...), custom_call_target="tpu_custom_call" | custom-call | tf_op jit(solution)/shard_map/pallas_call | solution.py:295
  (29 shorter events, 1.3 us)
Async XLA Ops:
  0.6 1.0 %copy-start = (f32[2,4,8,12,128]{4,2,3,1,0:T(8,128)S(1)}, f32[2,4,8,12,128]{4,2,3,1,0:T(8,128)}, u32[]{:S(2)}) copy-start(f32[2,4,8,12,128]{4,2,3,1,0:T(8,128)} %param.2) | copy-start | bytes 1179652
  1.8 23.3 %collective-permute-start = (f32[96,8,128]{2,1,0:T(8,128)S(1)}, f32[96,8,128]{2,1,0:T(8,128)S(1)}, u32[]{:S(2)}, u32[]{:S(2)}) collective-permute-start(f32[96,8,128]{2,1,0:T(8,128)S(1)} %get-tuple-element.20.refs_0_), channel_id=1, source_target_pairs={{0,16},{1,17},{2,18},{3,19},{4,20},{5,21},{6,22},{7,23},{8,24},{9,... | collective-permute-start | bytes 1179656 | tf_op jit(solution)/shard_map/ppermute | solution.py:60
  3.3 3.2 %collective-permute-start.5 = (f32[12,8,128]{2,1,0:T(8,128)S(1)}, f32[12,8,128]{2,1,0:T(8,128)S(1)}, u32[]{:S(2)}, u32[]{:S(2)}) collective-permute-start(f32[12,8,128]{2,1,0:T(8,128)S(1)} %get-tuple-element.25), channel_id=1, source_target_pairs={{0,1},{1,0},{2,3},{3,2},{4,5},{5,4},{6,7},{7,6},{8,9},{9,8},{10,11... | collective-permute-start | bytes 147464 | tf_op jit(solution)/shard_map/ppermute | solution.py:60
  3.3 21.8 %collective-permute-start.1 = (f32[64,8,128]{2,1,0:T(8,128)S(1)}, f32[64,8,128]{2,1,0:T(8,128)S(1)}, u32[]{:S(2)}, u32[]{:S(2)}) collective-permute-start(f32[64,8,128]{2,1,0:T(8,128)S(1)} %get-tuple-element.21), channel_id=1, source_target_pairs={{0,4},{1,5},{2,6},{3,7},{4,0},{5,1},{6,2},{7,3},{8,12},{9,13},{10,... | collective-permute-start | bytes 786440 | tf_op jit(solution)/shard_map/ppermute | solution.py:60
  3.8 6.9 %copy-start.1 = (f32[8,12,128]{2,0,1:T(8,128)S(1)}, f32[8,12,128]{2,0,1:T(8,128)}, u32[]{:S(2)}) copy-start(f32[8,12,128]{2,0,1:T(8,128)} %param.3) | copy-start | bytes 147460
  3.8 21.3 %collective-permute-start.2 = (f32[64,8,128]{2,1,0:T(8,128)S(1)}, f32[64,8,128]{2,1,0:T(8,128)S(1)}, u32[]{:S(2)}, u32[]{:S(2)}) collective-permute-start(f32[64,8,128]{2,1,0:T(8,128)S(1)} %get-tuple-element.22), channel_id=1, source_target_pairs={{0,1},{1,0},{2,3},{3,2},{4,8},{5,9},{6,10},{7,11},{8,4},{9,5},{10,... | collective-permute-start | bytes 786440 | tf_op jit(solution)/shard_map/ppermute | solution.py:60
  6.5 4.2 %collective-permute-start.6 = (f32[12,8,128]{2,1,0:T(8,128)S(1)}, f32[12,8,128]{2,1,0:T(8,128)S(1)}, u32[]{:S(2)}, u32[]{:S(2)}) collective-permute-start(f32[12,8,128]{2,1,0:T(8,128)S(1)} %add.6.refs_0_), channel_id=1, source_target_pairs={{0,2},{1,3},{2,0},{3,1},{4,6},{5,7},{6,4},{7,5},{8,10},{9,11},{10,... | collective-permute-start | bytes 147464 | tf_op jit(solution)/shard_map/ppermute | solution.py:60
  10.7 4.5 %collective-permute-start.7 = (f32[12,8,128]{2,1,0:T(8,128)S(1)}, f32[12,8,128]{2,1,0:T(8,128)S(1)}, u32[]{:S(2)}, u32[]{:S(2)}) collective-permute-start(f32[12,8,128]{2,1,0:T(8,128)S(1)} %shard_map.42.v_here.refs_6_), channel_id=1, source_target_pairs={{0,16},{1,17},{2,18},{3,19},{4,20},{5,21},{6,22},{7,23},{8,24},{9,... | collective-permute-start | bytes 147464 | tf_op jit(solution)/shard_map/ppermute | solution.py:60
  11.3 7.1 %collective-permute-start.3 = (f32[24,8,128]{2,1,0:T(8,128)S(1)}, f32[24,8,128]{2,1,0:T(8,128)S(1)}, u32[]{:S(2)}, u32[]{:S(2)}) collective-permute-start(f32[24,8,128]{2,1,0:T(8,128)S(1)} %get-tuple-element.23), channel_id=1, source_target_pairs={{0,20},{1,21},{2,22},{3,23},{4,16},{5,17},{6,18},{7,19},{8,28},{9,... | collective-permute-start | bytes 294920 | tf_op jit(solution)/shard_map/ppermute | solution.py:60
  15.2 5.8 %collective-permute-start.4 = (f32[24,8,128]{2,1,0:T(8,128)S(1)}, f32[24,8,128]{2,1,0:T(8,128)S(1)}, u32[]{:S(2)}, u32[]{:S(2)}) collective-permute-start(f32[24,8,128]{2,1,0:T(8,128)S(1)} %get-tuple-element.24), channel_id=1, source_target_pairs={{0,1},{1,0},{2,3},{3,2},{4,24},{5,25},{6,26},{7,27},{8,20},{9,21},... | collective-permute-start | bytes 294920 | tf_op jit(solution)/shard_map/ppermute | solution.py:60
  18.4 4.6 %collective-permute-start.8 = (f32[12,8,128]{2,1,0:T(8,128)S(1)}, f32[12,8,128]{2,1,0:T(8,128)S(1)}, u32[]{:S(2)}, u32[]{:S(2)}) collective-permute-start(f32[12,8,128]{2,1,0:T(8,128)S(1)} %get-tuple-element.26), channel_id=1, source_target_pairs={{0,4},{1,5},{2,6},{3,7},{4,0},{5,1},{6,2},{7,3},{8,12},{9,13},{10,... | collective-permute-start | bytes 147464 | tf_op jit(solution)/shard_map/ppermute | solution.py:60
  21.0 4.1 %collective-permute-start.9 = (f32[12,8,128]{2,1,0:T(8,128)S(1)}, f32[12,8,128]{2,1,0:T(8,128)S(1)}, u32[]{:S(2)}, u32[]{:S(2)}) collective-permute-start(f32[12,8,128]{2,1,0:T(8,128)S(1)} %get-tuple-element.27), channel_id=1, source_target_pairs={{0,1},{1,0},{2,3},{3,2},{4,8},{5,9},{6,10},{7,11},{8,4},{9,5},{10,... | collective-permute-start | bytes 147464 | tf_op jit(solution)/shard_map/ppermute | solution.py:60
  29.5 22.4 %collective-permute-start.10 = (f32[96,8,128]{2,1,0:T(8,128)S(1)}, f32[96,8,128]{2,1,0:T(8,128)S(1)}, u32[]{:S(2)}, u32[]{:S(2)}) collective-permute-start(f32[96,8,128]{2,1,0:T(8,128)S(1)} %get-tuple-element.28.refs_0_), channel_id=1, source_target_pairs={{0,16},{1,17},{2,18},{3,19},{4,20},{5,21},{6,22},{7,23},{8,24},{9,... | collective-permute-start | bytes 1179656 | tf_op jit(solution)/shard_map/ppermute | solution.py:60
  31.5 2.0 %collective-permute-start.15 = (f32[12,8,128]{2,1,0:T(8,128)S(1)}, f32[12,8,128]{2,1,0:T(8,128)S(1)}, u32[]{:S(2)}, u32[]{:S(2)}) collective-permute-start(f32[12,8,128]{2,1,0:T(8,128)S(1)} %get-tuple-element.33), channel_id=1, source_target_pairs={{0,1},{1,0},{2,3},{3,2},{4,5},{5,4},{6,7},{7,6},{8,9},{9,8},{10,11... | collective-permute-start | bytes 147464 | tf_op jit(solution)/shard_map/ppermute | solution.py:60
  31.5 20.4 %collective-permute-start.11 = (f32[64,8,128]{2,1,0:T(8,128)S(1)}, f32[64,8,128]{2,1,0:T(8,128)S(1)}, u32[]{:S(2)}, u32[]{:S(2)}) collective-permute-start(f32[64,8,128]{2,1,0:T(8,128)S(1)} %get-tuple-element.29), channel_id=1, source_target_pairs={{0,4},{1,5},{2,6},{3,7},{4,0},{5,1},{6,2},{7,3},{8,12},{9,13},{10,... | collective-permute-start | bytes 786440 | tf_op jit(solution)/shard_map/ppermute | solution.py:60
  31.5 20.4 %collective-permute-start.12 = (f32[64,8,128]{2,1,0:T(8,128)S(1)}, f32[64,8,128]{2,1,0:T(8,128)S(1)}, u32[]{:S(2)}, u32[]{:S(2)}) collective-permute-start(f32[64,8,128]{2,1,0:T(8,128)S(1)} %get-tuple-element.30), channel_id=1, source_target_pairs={{0,1},{1,0},{2,3},{3,2},{4,8},{5,9},{6,10},{7,11},{8,4},{9,5},{10,... | collective-permute-start | bytes 786440 | tf_op jit(solution)/shard_map/ppermute | solution.py:60
  33.5 4.2 %collective-permute-start.16 = (f32[12,8,128]{2,1,0:T(8,128)S(1)}, f32[12,8,128]{2,1,0:T(8,128)S(1)}, u32[]{:S(2)}, u32[]{:S(2)}) collective-permute-start(f32[12,8,128]{2,1,0:T(8,128)S(1)} %add.7.refs_0_), channel_id=1, source_target_pairs={{0,2},{1,3},{2,0},{3,1},{4,6},{5,7},{6,4},{7,5},{8,10},{9,11},{10,... | collective-permute-start | bytes 147464 | tf_op jit(solution)/shard_map/ppermute | solution.py:60
  37.7 4.6 %collective-permute-start.17 = (f32[12,8,128]{2,1,0:T(8,128)S(1)}, f32[12,8,128]{2,1,0:T(8,128)S(1)}, u32[]{:S(2)}, u32[]{:S(2)}) collective-permute-start(f32[12,8,128]{2,1,0:T(8,128)S(1)} %shard_map.45.v_here.refs_6_), channel_id=1, source_target_pairs={{0,16},{1,17},{2,18},{3,19},{4,20},{5,21},{6,22},{7,23},{8,24},{9,... | collective-permute-start | bytes 147464 | tf_op jit(solution)/shard_map/ppermute | solution.py:60
  38.0 5.5 %collective-permute-start.13 = (f32[24,8,128]{2,1,0:T(8,128)S(1)}, f32[24,8,128]{2,1,0:T(8,128)S(1)}, u32[]{:S(2)}, u32[]{:S(2)}) collective-permute-start(f32[24,8,128]{2,1,0:T(8,128)S(1)} %get-tuple-element.31), channel_id=1, source_target_pairs={{0,20},{1,21},{2,22},{3,23},{4,16},{5,17},{6,18},{7,19},{8,28},{9,... | collective-permute-start | bytes 294920 | tf_op jit(solution)/shard_map/ppermute | solution.py:60
  42.3 5.5 %collective-permute-start.14 = (f32[24,8,128]{2,1,0:T(8,128)S(1)}, f32[24,8,128]{2,1,0:T(8,128)S(1)}, u32[]{:S(2)}, u32[]{:S(2)}) collective-permute-start(f32[24,8,128]{2,1,0:T(8,128)S(1)} %get-tuple-element.32), channel_id=1, source_target_pairs={{0,1},{1,0},{2,3},{3,2},{4,24},{5,25},{6,26},{7,27},{8,20},{9,21},... | collective-permute-start | bytes 294920 | tf_op jit(solution)/shard_map/ppermute | solution.py:60
  43.5 5.4 %collective-permute-start.18 = (f32[12,8,128]{2,1,0:T(8,128)S(1)}, f32[12,8,128]{2,1,0:T(8,128)S(1)}, u32[]{:S(2)}, u32[]{:S(2)}) collective-permute-start(f32[12,8,128]{2,1,0:T(8,128)S(1)} %get-tuple-element.34), channel_id=1, source_target_pairs={{0,4},{1,5},{2,6},{3,7},{4,0},{5,1},{6,2},{7,3},{8,12},{9,13},{10,... | collective-permute-start | bytes 147464 | tf_op jit(solution)/shard_map/ppermute | solution.py:60
  47.8 4.1 %collective-permute-start.19 = (f32[12,8,128]{2,1,0:T(8,128)S(1)}, f32[12,8,128]{2,1,0:T(8,128)S(1)}, u32[]{:S(2)}, u32[]{:S(2)}) collective-permute-start(f32[12,8,128]{2,1,0:T(8,128)S(1)} %get-tuple-element.35), channel_id=1, source_target_pairs={{0,1},{1,0},{2,3},{3,2},{4,8},{5,9},{6,10},{7,11},{8,4},{9,5},{10,... | collective-permute-start | bytes 147464 | tf_op jit(solution)/shard_map/ppermute | solution.py:60
where the time goes:
time: 57.2 us; the launch traced here: 57 us
  waiting for transfers between devices  26.5 us (46%)
  starting transfers between devices  19.1 us (33%)
  Pallas kernels  9.68 us (17%)
  local copies, waits for them, and re-layouts  0.99 us (2%)
  between operations  0.7 us (1%)
    ppermute x20, waiting for transfers between devices, swap(): return lax.ppermute(value, AXES, self.pairs(**kinds))  26.5 us
    ppermute x20, starting transfers between devices, swap(): return lax.ppermute(value, AXES, self.pairs(**kinds))  19.1 us
    pallas_call x7, Pallas kernels, call(): pl.pallas_call(kernel, out_shape=[jax.ShapeDtypeStruct(s, jnp.float32) fo...  9.68 us
  transfers between devices with their start and end apart: 20, of which 9 were waited for; matrix products, arithmetic and copies ran while one was open for 0% of the time, Pallas kernels for 0%

commit v1 on v0

--- a/solution.py
+++ b/solution.py
@@ -41,7 +41,11 @@
         self.ext_cols = self.cols + 2 * WIDE
         self.corner = sum(corner_depth(d) for d in range(1, WIDE - 1))
         self.v_cols = WIDE // 2
-        self.edge_cells = len(self.xs) * self.v_cols + WIDE
+        self.edge_cells = len(self.xs) * (self.corner + self.v_cols) + WIDE
+        depth = [min(c + 1, self.cols - c) for c in range(self.cols)]
+        self.soon = [corner_depth(d) if d < WIDE - 1 else 0 for d in depth]
+        self.soon_at = [sum(self.soon[:c]) for c in range(self.cols + 1)]
+        self.late_at = [c * WIDE - self.soon_at[c] for c in range(self.cols + 1)]
         self.wide_cells = WIDE * self.rows
 
     def pairs(self, kx=None, ky=None, flip=0):
@@ -80,20 +84,19 @@
 
 
 def pack(plan, fields_ref, out_refs):
-    out_refs = list(out_refs)
-    for ky in plan.ys:
-        base, out = plan.near(plan.above("gy", ky), WIDE, plan.cols), out_refs.pop(0)
+    nx, ny = len(plan.xs), len(plan.ys)
+    rows = plan.rows
+    for ky, out in zip(plan.ys, out_refs[:ny]):
+        base = plan.near(plan.above("gy", ky), WIDE, plan.cols)
         for c in range(WIDE):
-            out[pl.ds(c * plan.rows, plan.rows)] = fields_ref[pl.ds((base + c) * plan.rows, plan.rows)]
-    for ky in plan.ys:
-        hi = plan.above("gy", ky)
-        for kx in plan.xs:
-            x_hi, out, at = plan.above("gx", kx), out_refs.pop(0), 0
-            for d in range(1, WIDE - 1):
-                size = corner_depth(d)
-                col = jnp.where(hi, plan.cols - d, d - 1)
-                out[at : at + size] = fields_ref[pl.ds(col * plan.rows + plan.near(x_hi, size, plan.rows), size)]
-                at += size
+            out[pl.ds(c * rows, rows)] = fields_ref[pl.ds((base + c) * rows, rows)]
+    for kx, soon, late in zip(plan.xs, out_refs[ny : ny + nx], out_refs[ny + nx :]):
+        hi = plan.above("gx", kx)
+        for c, n in enumerate(plan.soon):
+            if n:
+                soon[plan.soon_at[c] : plan.soon_at[c + 1]] = fields_ref[pl.ds(c * rows + plan.near(hi, n, rows), n)]
+            first = c * rows + jnp.where(hi, rows - WIDE, n)
+            late[plan.late_at[c] : plan.late_at[c + 1]] = fields_ref[pl.ds(first, WIDE - n)]
 
 
 def enter_kernel(plan, orb_ref, fields_ref, dens_ref, *rest):
@@ -129,13 +132,16 @@
 
 def edge_kernel(plan, v_here, *refs):
     nx = len(plan.xs)
-    v_there, out = refs[:nx], refs[nx:]
+    v_there, soon, out = refs[:nx], refs[nx : 2 * nx], refs[2 * nx :]
     for ky, o in zip(plan.ys, out):
         hi = plan.above("gy", ky)
         o[0:WIDE] = v_here[pl.ds(plan.near(hi, WIDE, plan.cols), WIDE)]
         for n in range(nx):
-            at = WIDE + n * plan.v_cols
+            at = WIDE + n * (plan.v_cols + plan.corner)
             o[at : at + plan.v_cols] = v_there[n][pl.ds(plan.near(hi, plan.v_cols, plan.cols), plan.v_cols)]
+            at += plan.v_cols
+            base = jnp.where(hi, plan.soon_at[-1] - plan.corner, 0)
+            o[at : at + plan.corner] = soon[n][pl.ds(base, plan.corner)]
 
 
 def evolve_kernel(plan, final, *refs):
@@ -143,15 +149,14 @@
     refs = list(refs)
     take = lambda n: [refs.pop(0) for _ in range(n)]
     (own,) = take(1)
-    far, big = take(nx), take(ny)
-    corners = [take(nx) for _ in range(ny)]
+    soon, late, big, edge = take(nx), take(nx), take(ny), take(ny)
     (v_here,) = take(1)
-    v_there, edge = take(nx), take(ny)
+    v_there = take(nx)
     if final:
         orb_ref, v_out = take(2)
     else:
         (half_ref, dens_ref) = take(2)
-        packed = take(ny + nx * ny)
+        packed = take(ny + 2 * nx)
     levels = take(ORDER)
     (pot,) = take(1)
     if final:
@@ -175,7 +180,11 @@
         row, src = plan.beyond(x_hi, WIDE, rows), plan.at_partner(x_hi, WIDE, rows)
         for c in range(cols):
             at = (WIDE + c) * long + row
-            h0[pl.ds(at, WIDE)] = far[n][pl.ds(c * rows + src, WIDE)]
+            size = plan.soon[c]
+            if size:
+                first = (WIDE + c) * long + plan.beyond(x_hi, size, rows)
+                h0[pl.ds(first, size)] = soon[n][plan.soon_at[c] : plan.soon_at[c + 1]]
+            h0[pl.ds(at + jnp.where(x_hi, size, 0), WIDE - size)] = late[n][plan.late_at[c] : plan.late_at[c + 1]]
             put_potential(at, v_there[n][c, pl.ds(src, WIDE), :], WIDE)
     for n, ky in enumerate(plan.ys):
         hi = plan.above("gy", ky)
@@ -185,18 +194,18 @@
             h0[pl.ds(at, rows)] = big[n][pl.ds(c * rows, rows)]
             put_potential(at, edge[n][c], rows)
         for n_x, kx in enumerate(plan.xs):
-            at = WIDE + n_x * plan.v_cols
+            at = WIDE + n_x * (plan.v_cols + plan.corner)
             x_hi = plan.above("gx", kx)
             row, src = plan.beyond(x_hi, WIDE, rows), plan.at_partner(x_hi, WIDE, rows)
             first = plan.beyond(hi, plan.v_cols, cols)
             for c in range(plan.v_cols):
                 put_potential((first + c) * long + row, edge[n][at + c, pl.ds(src, WIDE), :], WIDE)
-            at = 0
+            at += plan.v_cols
             for d in range(1, WIDE - 1):
                 size = corner_depth(d)
+                there = jnp.where(hi, plan.soon_at[d - 1], plan.corner - plan.soon_at[d])
                 col = jnp.where(hi, WIDE + cols + d - 1, WIDE - d)
-                h0[pl.ds(col * long + plan.beyond(x_hi, size, rows), size)] = corners[n][n_x][at : at + size]
-                at += size
+                h0[pl.ds(col * long + plan.beyond(x_hi, size, rows), size)] = edge[n][pl.ds(at + there, size)]
 
     def clear_outside(h):
         for outside, col in ((j == 0, WIDE - 2), (j == plan.gy - 1, WIDE + cols)):
@@ -310,7 +319,8 @@
         field_shape, plane = (cells, f, LANES), (plan.cols, plan.rows, LANES)
         wide = (plan.wide_cells, f, LANES)
         nx, ny = len(plan.xs), len(plan.ys)
-        packed = [wide] * ny + [(plan.corner, f, LANES)] * (nx * ny)
+        soon, late = plan.soon_at[-1], plan.late_at[-1]
+        packed = [wide] * ny + [(soon, f, LANES)] * nx + [(late, f, LANES)] * nx
 
         fields, dens, *out = call(
             functools.partial(enter_kernel, plan),
@@ -318,31 +328,30 @@
             [pltpu.VMEM((cells * f, LANES), jnp.float32)],
         )(orbitals)
 
-        def gather(fields, dens, out):
+        def gather(dens, out):
             def swap(value, **kinds):
                 return plan.swap(value, **kinds)
 
-            far = [swap(fields, kx=k) for k in plan.xs]
             big = [swap(v, ky=k) for k, v in zip(plan.ys, out)]
-            both = [(ky, kx) for ky in plan.ys for kx in plan.xs]
-            corners = [swap(v, kx=kx, ky=ky) for (ky, kx), v in zip(both, out[ny:])]
+            soon = [swap(v, kx=k) for k, v in zip(plan.xs, out[ny:])]
+            late = [swap(v, kx=k) for k, v in zip(plan.xs, out[ny + nx :])]
             dens = dens + swap(dens, flip=1)
             more = [swap(dens, flip=b) for b in range(2, plan.groups, 2)]
             (v_here,) = call(potential_kernel, [plane])(external, dens, *more)
             v_there = [swap(v_here, kx=k) for k in plan.xs]
             edge = call(
-                functools.partial(edge_kernel, plan), [(plan.edge_cells, plan.rows, LANES)] * ny
-            )(v_here, *v_there)
+                functools.partial(edge_kernel, plan), [(plan.edge_cells, f, LANES)] * ny
+            )(v_here, *v_there, *soon)
             edge = [swap(v, ky=k) for k, v in zip(plan.ys, edge)]
-            return [*far, *big, *corners, v_here, *v_there, *edge]
+            return [*soon, *late, *big, *edge, v_here, *v_there]
 
         extended = pltpu.VMEM((plan.ext_rows * plan.ext_cols, f, LANES), jnp.float32)
         scratch = [extended] * (ORDER + 1)
-        arrived = gather(fields, dens, out)
+        arrived = gather(dens, out)
         half, dens, *out = call(
             functools.partial(evolve_kernel, plan, False), [field_shape, plane] + packed, scratch, limit=24
         )(fields, *arrived)
-        arrived = gather(half, dens, out)
+        arrived = gather(dens, out)
         result, potential = call(
             functools.partial(evolve_kernel, plan, True),
             [orbitals.shape, plane],

time: 57.2 us -> 48.4 us (0.85)
  the two profiles are of different devices: /device:TPU:12 before, /device:TPU:0 now
where the time goes in v1:
time: 48.4 us; the launch traced here: 48.2 us
  starting transfers between devices  19.1 us (39%)
  waiting for transfers between devices  17.6 us (36%)
  Pallas kernels  9.79 us (20%)
  local copies, waits for them, and re-layouts  0.99 us (2%)
  between operations  0.7 us (1%)
    ppermute x18, starting transfers between devices, swap(): return lax.ppermute(value, AXES, self.pairs(**kinds))  19.1 us
    ppermute x18, waiting for transfers between devices, swap(): return lax.ppermute(value, AXES, self.pairs(**kinds))  17.6 us
    pallas_call x7, Pallas kernels, call(): pl.pallas_call(kernel, out_shape=[jax.ShapeDtypeStruct(s, jnp.float32) fo...  9.79 us
    unnamed x4, local copies, waits for them, and re-layouts  0.99 us
  transfers between devices with their start and end apart: 18, of which 7 were waited for; matrix products, arithmetic and copies ran while one was open for 0% of the time, Pallas kernels for 0%

profile of v1, /device:TPU:0, one launch (start us, length us, event | category | flops | bytes accessed | tf_op | source)
XLA Modules:
  0.0 48.2 jit_solution(4524520782801015640)
XLA Ops:
  0.6 1.0 %copy-done = f32[2,4,8,12,128]{4,2,3,1,0:T(8,128)S(1)} copy-done((f32[2,4,8,12,128]{4,2,3,1,0:T(8,128)S(1)}, f32[2,4,8,12,128]{4,2,3,1,0:T(8,128)}, u32[]{:S(2)}) %copy-start) | copy-done | bytes 393240
  1.8 3.0 %collective-permute-start = (f32[48,8,128]{2,1,0:T(8,128)S(1)}, f32[48,8,128]{2,1,0:T(8,128)S(1)}, u32[]{:S(2)}, u32[]{:S(2)}) collective-permute-start(f32[48,8,128]{2,1,0:T(8,128)S(1)} %get-tuple-element.21), channel_id=1, source_target_pairs={{0,16},{1,17},{2,18},{3,19},{4,20},{5,21},{6,22},{7,23},{8,24},{9,... | collective-permute-start | bytes 589832 | tf_op jit(solution)/shard_map/ppermute | solution.py:64
  4.8 1.6 %collective-permute-start.2 = (f32[64,8,128]{2,1,0:T(8,128)S(1)}, f32[64,8,128]{2,1,0:T(8,128)S(1)}, u32[]{:S(2)}, u32[]{:S(2)}) collective-permute-start(f32[64,8,128]{2,1,0:T(8,128)S(1)} %get-tuple-element.23), channel_id=1, source_target_pairs={{0,4},{1,5},{2,6},{3,7},{4,0},{5,1},{6,2},{7,3},{8,12},{9,13},{10,... | collective-permute-start | bytes 786440 | tf_op jit(solution)/shard_map/ppermute | solution.py:64
  6.4 0.2 collective-permute-start.3
  6.6 1.6 %collective-permute-start.5 = (f32[12,8,128]{2,1,0:T(8,128)S(1)}, f32[12,8,128]{2,1,0:T(8,128)S(1)}, u32[]{:S(2)}, u32[]{:S(2)}) collective-permute-start(f32[12,8,128]{2,1,0:T(8,128)S(1)} %add.6.refs_0_), channel_id=1, source_target_pairs={{0,2},{1,3},{2,0},{3,1},{4,6},{5,7},{6,4},{7,5},{8,10},{9,11},{10,... | collective-permute-start | bytes 147464 | tf_op jit(solution)/shard_map/ppermute | solution.py:64
  8.2 2.6 %collective-permute-done.5.refs_1_ = f32[12,8,128]{2,1,0:T(8,128)S(1)} collective-permute-done((f32[12,8,128]{2,1,0:T(8,128)S(1)}, f32[12,8,128]{2,1,0:T(8,128)S(1)}, u32[]{:S(2)}, u32[]{:S(2)}) %collective-permute-start.5) | collective-permute-done | bytes 49184 | tf_op jit(solution)/shard_map/ppermute | solution.py:64
  10.8 0.6 %collective-permute-start.6 = (f32[12,8,128]{2,1,0:T(8,128)S(1)}, f32[12,8,128]{2,1,0:T(8,128)S(1)}, u32[]{:S(2)}, u32[]{:S(2)}) collective-permute-start(f32[12,8,128]{2,1,0:T(8,128)S(1)} %shard_map.42.v_here.refs_7_), channel_id=1, source_target_pairs={{0,16},{1,17},{2,18},{3,19},{4,20},{5,21},{6,22},{7,23},{8,24},{9,... | collective-permute-start | bytes 147464 | tf_op jit(solution)/shard_map/ppermute | solution.py:64
  11.4 1.5 %collective-permute-start.1 = (f32[48,8,128]{2,1,0:T(8,128)S(1)}, f32[48,8,128]{2,1,0:T(8,128)S(1)}, u32[]{:S(2)}, u32[]{:S(2)}) collective-permute-start(f32[48,8,128]{2,1,0:T(8,128)S(1)} %get-tuple-element.22), channel_id=1, source_target_pairs={{0,16},{1,17},{2,18},{3,19},{4,20},{5,21},{6,22},{7,23},{8,24},{9,... | collective-permute-start | bytes 589832 | tf_op jit(solution)/shard_map/ppermute | solution.py:64
  12.9 2.6 %collective-permute-done.6.refs_0_.refs_8_ = f32[12,8,128]{2,1,0:T(8,128)S(1)} collective-permute-done((f32[12,8,128]{2,1,0:T(8,128)S(1)}, f32[12,8,128]{2,1,0:T(8,128)S(1)}, u32[]{:S(2)}, u32[]{:S(2)}) %collective-permute-start.6) | collective-permute-done | bytes 49184 | tf_op jit(solution)/shard_map/ppermute | solution.py:64
  15.6 3.0 %collective-permute-start.7 = (f32[36,8,128]{2,1,0:T(8,128)S(1)}, f32[36,8,128]{2,1,0:T(8,128)S(1)}, u32[]{:S(2)}, u32[]{:S(2)}) collective-permute-start(f32[36,8,128]{2,1,0:T(8,128)S(1)} %get-tuple-element.26), channel_id=1, source_target_pairs={{0,4},{1,5},{2,6},{3,7},{4,0},{5,1},{6,2},{7,3},{8,12},{9,13},{10,... | collective-permute-start | bytes 442376 | tf_op jit(solution)/shard_map/ppermute | solution.py:64
  18.6 3.1 %collective-permute-done.7.refs_5_ = f32[36,8,128]{2,1,0:T(8,128)S(1)} collective-permute-done((f32[36,8,128]{2,1,0:T(8,128)S(1)}, f32[36,8,128]{2,1,0:T(8,128)S(1)}, u32[]{:S(2)}, u32[]{:S(2)}) %collective-permute-start.7) | collective-permute-done | bytes 147488 | tf_op jit(solution)/shard_map/ppermute | solution.py:64
  21.7 4.4 %shard_map.44 = (f32[96,8,128]{2,1,0:T(8,128)S(1)}, f32[12,8,128]{2,1,0:T(8,128)S(1)}, f32[64,8,128]{2,1,0:T(8,128)S(1)}, f32[64,8,128]{2,1,0:T(8,128)S(1)}, f32...) custom-call(f32[96,8,128]{2,1,0:T(8,128)S(1)} %get-tuple-element.20.refs_0_, ...), custom_call_target="tpu_custom_call" | custom-call | tf_op jit(solution)/shard_map/pallas_call | solution.py:304
  26.1 0.6 %collective-permute-start.9 = (f32[48,8,128]{2,1,0:T(8,128)S(1)}, f32[48,8,128]{2,1,0:T(8,128)S(1)}, u32[]{:S(2)}, u32[]{:S(2)}) collective-permute-start(f32[48,8,128]{2,1,0:T(8,128)S(1)} %get-tuple-element.29), channel_id=1, source_target_pairs={{0,16},{1,17},{2,18},{3,19},{4,20},{5,21},{6,22},{7,23},{8,24},{9,... | collective-permute-start | bytes 589832 | tf_op jit(solution)/shard_map/ppermute | solution.py:64
  26.7 2.1 %collective-permute-start.11 = (f32[64,8,128]{2,1,0:T(8,128)S(1)}, f32[64,8,128]{2,1,0:T(8,128)S(1)}, u32[]{:S(2)}, u32[]{:S(2)}) collective-permute-start(f32[64,8,128]{2,1,0:T(8,128)S(1)} %get-tuple-element.31), channel_id=1, source_target_pairs={{0,4},{1,5},{2,6},{3,7},{4,0},{5,1},{6,2},{7,3},{8,12},{9,13},{10,... | collective-permute-start | bytes 786440 | tf_op jit(solution)/shard_map/ppermute | solution.py:64
  28.8 0.2 collective-permute-start.12
  29.0 1.6 %collective-permute-start.14 = (f32[12,8,128]{2,1,0:T(8,128)S(1)}, f32[12,8,128]{2,1,0:T(8,128)S(1)}, u32[]{:S(2)}, u32[]{:S(2)}) collective-permute-start(f32[12,8,128]{2,1,0:T(8,128)S(1)} %add.7.refs_0_), channel_id=1, source_target_pairs={{0,2},{1,3},{2,0},{3,1},{4,6},{5,7},{6,4},{7,5},{8,10},{9,11},{10,... | collective-permute-start | bytes 147464 | tf_op jit(solution)/shard_map/ppermute | solution.py:64
  30.6 2.6 %collective-permute-done.14.refs_1_ = f32[12,8,128]{2,1,0:T(8,128)S(1)} collective-permute-done((f32[12,8,128]{2,1,0:T(8,128)S(1)}, f32[12,8,128]{2,1,0:T(8,128)S(1)}, u32[]{:S(2)}, u32[]{:S(2)}) %collective-permute-start.14) | collective-permute-done | bytes 49184 | tf_op jit(solution)/shard_map/ppermute | solution.py:64
  33.2 1.6 %collective-permute-start.15 = (f32[12,8,128]{2,1,0:T(8,128)S(1)}, f32[12,8,128]{2,1,0:T(8,128)S(1)}, u32[]{:S(2)}, u32[]{:S(2)}) collective-permute-start(f32[12,8,128]{2,1,0:T(8,128)S(1)} %shard_map.45.v_here.refs_7_), channel_id=1, source_target_pairs={{0,16},{1,17},{2,18},{3,19},{4,20},{5,21},{6,22},{7,23},{8,24},{9,... | collective-permute-start | bytes 147464 | tf_op jit(solution)/shard_map/ppermute | solution.py:64
  34.8 0.5 %collective-permute-start.10 = (f32[48,8,128]{2,1,0:T(8,128)S(1)}, f32[48,8,128]{2,1,0:T(8,128)S(1)}, u32[]{:S(2)}, u32[]{:S(2)}) collective-permute-start(f32[48,8,128]{2,1,0:T(8,128)S(1)} %get-tuple-element.30), channel_id=1, source_target_pairs={{0,16},{1,17},{2,18},{3,19},{4,20},{5,21},{6,22},{7,23},{8,24},{9,... | collective-permute-start | bytes 589832 | tf_op jit(solution)/shard_map/ppermute | solution.py:64
  35.3 2.6 %collective-permute-done.15.refs_0_.refs_8_ = f32[12,8,128]{2,1,0:T(8,128)S(1)} collective-permute-done((f32[12,8,128]{2,1,0:T(8,128)S(1)}, f32[12,8,128]{2,1,0:T(8,128)S(1)}, u32[]{:S(2)}, u32[]{:S(2)}) %collective-permute-start.15) | collective-permute-done | bytes 49184 | tf_op jit(solution)/shard_map/ppermute | solution.py:64
  37.9 1.1 %collective-permute-start.16 = (f32[36,8,128]{2,1,0:T(8,128)S(1)}, f32[36,8,128]{2,1,0:T(8,128)S(1)}, u32[]{:S(2)}, u32[]{:S(2)}) collective-permute-start(f32[36,8,128]{2,1,0:T(8,128)S(1)} %get-tuple-element.34), channel_id=1, source_target_pairs={{0,4},{1,5},{2,6},{3,7},{4,0},{5,1},{6,2},{7,3},{8,12},{9,13},{10,... | collective-permute-start | bytes 442376 | tf_op jit(solution)/shard_map/ppermute | solution.py:64
  39.0 2.3 %collective-permute-done.10.refs_2_ = f32[48,8,128]{2,1,0:T(8,128)S(1)} collective-permute-done((f32[48,8,128]{2,1,0:T(8,128)S(1)}, f32[48,8,128]{2,1,0:T(8,128)S(1)}, u32[]{:S(2)}, u32[]{:S(2)}) %collective-permute-start.10) | collective-permute-done | bytes 196640 | tf_op jit(solution)/shard_map/ppermute | solution.py:64
  41.2 1.9 %collective-permute-done.16.refs_5_ = f32[36,8,128]{2,1,0:T(8,128)S(1)} collective-permute-done((f32[36,8,128]{2,1,0:T(8,128)S(1)}, f32[36,8,128]{2,1,0:T(8,128)S(1)}, u32[]{:S(2)}, u32[]{:S(2)}) %collective-permute-start.16) | collective-permute-done | bytes 147488 | tf_op jit(solution)/shard_map/ppermute | solution.py:64
  43.1 5.1 %shard_map.47 = (f32[2,4,12,8,128]{4,3,2,1,0:T(8,128)}, f32[12,8,128]{2,1,0:T(8,128)}) custom-call(f32[96,8,128]{2,1,0:T(8,128)S(1)} %get-tuple-element.28.refs_0_, f32[48,8,128]{2,1,0:T(8,128)S(1)} %collective-permute-done.9.refs_1_, f32[48,8,128]{2,1,0:T(8,128)S(1)} %collective-permute-done.10.refs_2_, f32[64,8,128]{2,1,0:T(8,128)S(1)} %collective-permute-done.11.refs_3_, ...), custom_call_target="tpu_custom_call" | custom-call | tf_op jit(solution)/shard_map/pallas_call | solution.py:304
  (25 shorter events, 0.3 us)
Async XLA Ops:
  0.6 1.0 %copy-start = (f32[2,4,8,12,128]{4,2,3,1,0:T(8,128)S(1)}, f32[2,4,8,12,128]{4,2,3,1,0:T(8,128)}, u32[]{:S(2)}) copy-start(f32[2,4,8,12,128]{4,2,3,1,0:T(8,128)} %param.2) | copy-start | bytes 1179652
  1.8 13.7 %collective-permute-start = (f32[48,8,128]{2,1,0:T(8,128)S(1)}, f32[48,8,128]{2,1,0:T(8,128)S(1)}, u32[]{:S(2)}, u32[]{:S(2)}) collective-permute-start(f32[48,8,128]{2,1,0:T(8,128)S(1)} %get-tuple-element.21), channel_id=1, source_target_pairs={{0,16},{1,17},{2,18},{3,19},{4,20},{5,21},{6,22},{7,23},{8,24},{9,... | collective-permute-start | bytes 589832 | tf_op jit(solution)/shard_map/ppermute | solution.py:64
  4.8 1.8 %collective-permute-start.4 = (f32[12,8,128]{2,1,0:T(8,128)S(1)}, f32[12,8,128]{2,1,0:T(8,128)S(1)}, u32[]{:S(2)}, u32[]{:S(2)}) collective-permute-start(f32[12,8,128]{2,1,0:T(8,128)S(1)} %get-tuple-element.25), channel_id=1, source_target_pairs={{0,1},{1,0},{2,3},{3,2},{4,5},{5,4},{6,7},{7,6},{8,9},{9,8},{10,11... | collective-permute-start | bytes 147464 | tf_op jit(solution)/shard_map/ppermute | solution.py:64
  4.8 13.7 %collective-permute-start.2 = (f32[64,8,128]{2,1,0:T(8,128)S(1)}, f32[64,8,128]{2,1,0:T(8,128)S(1)}, u32[]{:S(2)}, u32[]{:S(2)}) collective-permute-start(f32[64,8,128]{2,1,0:T(8,128)S(1)} %get-tuple-element.23), channel_id=1, source_target_pairs={{0,4},{1,5},{2,6},{3,7},{4,0},{5,1},{6,2},{7,3},{8,12},{9,13},{10,... | collective-permute-start | bytes 786440 | tf_op jit(solution)/shard_map/ppermute | solution.py:64
  6.4 4.4 %copy-start.1 = (f32[8,12,128]{2,0,1:T(8,128)S(1)}, f32[8,12,128]{2,0,1:T(8,128)}, u32[]{:S(2)}) copy-start(f32[8,12,128]{2,0,1:T(8,128)} %param.3) | copy-start | bytes 147460
  6.4 12.2 %collective-permute-start.3 = (f32[64,8,128]{2,1,0:T(8,128)S(1)}, f32[64,8,128]{2,1,0:T(8,128)S(1)}, u32[]{:S(2)}, u32[]{:S(2)}) collective-permute-start(f32[64,8,128]{2,1,0:T(8,128)S(1)} %get-tuple-element.24), channel_id=1, source_target_pairs={{0,1},{1,0},{2,3},{3,2},{4,8},{5,9},{6,10},{7,11},{8,4},{9,5},{10,... | collective-permute-start | bytes 786440 | tf_op jit(solution)/shard_map/ppermute | solution.py:64
  6.6 4.2 %collective-permute-start.5 = (f32[12,8,128]{2,1,0:T(8,128)S(1)}, f32[12,8,128]{2,1,0:T(8,128)S(1)}, u32[]{:S(2)}, u32[]{:S(2)}) collective-permute-start(f32[12,8,128]{2,1,0:T(8,128)S(1)} %add.6.refs_0_), channel_id=1, source_target_pairs={{0,2},{1,3},{2,0},{3,1},{4,6},{5,7},{6,4},{7,5},{8,10},{9,11},{10,... | collective-permute-start | bytes 147464 | tf_op jit(solution)/shard_map/ppermute | solution.py:64
  10.8 4.7 %collective-permute-start.6 = (f32[12,8,128]{2,1,0:T(8,128)S(1)}, f32[12,8,128]{2,1,0:T(8,128)S(1)}, u32[]{:S(2)}, u32[]{:S(2)}) collective-permute-start(f32[12,8,128]{2,1,0:T(8,128)S(1)} %shard_map.42.v_here.refs_7_), channel_id=1, source_target_pairs={{0,16},{1,17},{2,18},{3,19},{4,20},{5,21},{6,22},{7,23},{8,24},{9,... | collective-permute-start | bytes 147464 | tf_op jit(solution)/shard_map/ppermute | solution.py:64
  11.4 7.1 %collective-permute-start.1 = (f32[48,8,128]{2,1,0:T(8,128)S(1)}, f32[48,8,128]{2,1,0:T(8,128)S(1)}, u32[]{:S(2)}, u32[]{:S(2)}) collective-permute-start(f32[48,8,128]{2,1,0:T(8,128)S(1)} %get-tuple-element.22), channel_id=1, source_target_pairs={{0,16},{1,17},{2,18},{3,19},{4,20},{5,21},{6,22},{7,23},{8,24},{9,... | collective-permute-start | bytes 589832 | tf_op jit(solution)/shard_map/ppermute | solution.py:64
  15.6 6.1 %collective-permute-start.7 = (f32[36,8,128]{2,1,0:T(8,128)S(1)}, f32[36,8,128]{2,1,0:T(8,128)S(1)}, u32[]{:S(2)}, u32[]{:S(2)}) collective-permute-start(f32[36,8,128]{2,1,0:T(8,128)S(1)} %get-tuple-element.26), channel_id=1, source_target_pairs={{0,4},{1,5},{2,6},{3,7},{4,0},{5,1},{6,2},{7,3},{8,12},{9,13},{10,... | collective-permute-start | bytes 442376 | tf_op jit(solution)/shard_map/ppermute | solution.py:64
  18.5 3.1 %collective-permute-start.8 = (f32[36,8,128]{2,1,0:T(8,128)S(1)}, f32[36,8,128]{2,1,0:T(8,128)S(1)}, u32[]{:S(2)}, u32[]{:S(2)}) collective-permute-start(f32[36,8,128]{2,1,0:T(8,128)S(1)} %get-tuple-element.27), channel_id=1, source_target_pairs={{0,1},{1,0},{2,3},{3,2},{4,8},{5,9},{6,10},{7,11},{8,4},{9,5},{10,... | collective-permute-start | bytes 442376 | tf_op jit(solution)/shard_map/ppermute | solution.py:64
  26.1 11.8 %collective-permute-start.9 = (f32[48,8,128]{2,1,0:T(8,128)S(1)}, f32[48,8,128]{2,1,0:T(8,128)S(1)}, u32[]{:S(2)}, u32[]{:S(2)}) collective-permute-start(f32[48,8,128]{2,1,0:T(8,128)S(1)} %get-tuple-element.29), channel_id=1, source_target_pairs={{0,16},{1,17},{2,18},{3,19},{4,20},{5,21},{6,22},{7,23},{8,24},{9,... | collective-permute-start | bytes 589832 | tf_op jit(solution)/shard_map/ppermute | solution.py:64
  26.7 2.3 %collective-permute-start.13 = (f32[12,8,128]{2,1,0:T(8,128)S(1)}, f32[12,8,128]{2,1,0:T(8,128)S(1)}, u32[]{:S(2)}, u32[]{:S(2)}) collective-permute-start(f32[12,8,128]{2,1,0:T(8,128)S(1)} %get-tuple-element.33), channel_id=1, source_target_pairs={{0,1},{1,0},{2,3},{3,2},{4,5},{5,4},{6,7},{7,6},{8,9},{9,8},{10,11... | collective-permute-start | bytes 147464 | tf_op jit(solution)/shard_map/ppermute | solution.py:64
  26.7 14.5 %collective-permute-start.11 = (f32[64,8,128]{2,1,0:T(8,128)S(1)}, f32[64,8,128]{2,1,0:T(8,128)S(1)}, u32[]{:S(2)}, u32[]{:S(2)}) collective-permute-start(f32[64,8,128]{2,1,0:T(8,128)S(1)} %get-tuple-element.31), channel_id=1, source_target_pairs={{0,4},{1,5},{2,6},{3,7},{4,0},{5,1},{6,2},{7,3},{8,12},{9,13},{10,... | collective-permute-start | bytes 786440 | tf_op jit(solution)/shard_map/ppermute | solution.py:64
  28.8 12.5 %collective-permute-start.12 = (f32[64,8,128]{2,1,0:T(8,128)S(1)}, f32[64,8,128]{2,1,0:T(8,128)S(1)}, u32[]{:S(2)}, u32[]{:S(2)}) collective-permute-start(f32[64,8,128]{2,1,0:T(8,128)S(1)} %get-tuple-element.32), channel_id=1, source_target_pairs={{0,1},{1,0},{2,3},{3,2},{4,8},{5,9},{6,10},{7,11},{8,4},{9,5},{10,... | collective-permute-start | bytes 786440 | tf_op jit(solution)/shard_map/ppermute | solution.py:64
  29.0 4.2 %collective-permute-start.14 = (f32[12,8,128]{2,1,0:T(8,128)S(1)}, f32[12,8,128]{2,1,0:T(8,128)S(1)}, u32[]{:S(2)}, u32[]{:S(2)}) collective-permute-start(f32[12,8,128]{2,1,0:T(8,128)S(1)} %add.7.refs_0_), channel_id=1, source_target_pairs={{0,2},{1,3},{2,0},{3,1},{4,6},{5,7},{6,4},{7,5},{8,10},{9,11},{10,... | collective-permute-start | bytes 147464 | tf_op jit(solution)/shard_map/ppermute | solution.py:64
  33.2 4.7 %collective-permute-start.15 = (f32[12,8,128]{2,1,0:T(8,128)S(1)}, f32[12,8,128]{2,1,0:T(8,128)S(1)}, u32[]{:S(2)}, u32[]{:S(2)}) collective-permute-start(f32[12,8,128]{2,1,0:T(8,128)S(1)} %shard_map.45.v_here.refs_7_), channel_id=1, source_target_pairs={{0,16},{1,17},{2,18},{3,19},{4,20},{5,21},{6,22},{7,23},{8,24},{9,... | collective-permute-start | bytes 147464 | tf_op jit(solution)/shard_map/ppermute | solution.py:64
  34.8 6.5 %collective-permute-start.10 = (f32[48,8,128]{2,1,0:T(8,128)S(1)}, f32[48,8,128]{2,1,0:T(8,128)S(1)}, u32[]{:S(2)}, u32[]{:S(2)}) collective-permute-start(f32[48,8,128]{2,1,0:T(8,128)S(1)} %get-tuple-element.30), channel_id=1, source_target_pairs={{0,16},{1,17},{2,18},{3,19},{4,20},{5,21},{6,22},{7,23},{8,24},{9,... | collective-permute-start | bytes 589832 | tf_op jit(solution)/shard_map/ppermute | solution.py:64
  37.9 5.2 %collective-permute-start.16 = (f32[36,8,128]{2,1,0:T(8,128)S(1)}, f32[36,8,128]{2,1,0:T(8,128)S(1)}, u32[]{:S(2)}, u32[]{:S(2)}) collective-permute-start(f32[36,8,128]{2,1,0:T(8,128)S(1)} %get-tuple-element.34), channel_id=1, source_target_pairs={{0,4},{1,5},{2,6},{3,7},{4,0},{5,1},{6,2},{7,3},{8,12},{9,13},{10,... | collective-permute-start | bytes 442376 | tf_op jit(solution)/shard_map/ppermute | solution.py:64
  39.0 4.2 %collective-permute-start.17 = (f32[36,8,128]{2,1,0:T(8,128)S(1)}, f32[36,8,128]{2,1,0:T(8,128)S(1)}, u32[]{:S(2)}, u32[]{:S(2)}) collective-permute-start(f32[36,8,128]{2,1,0:T(8,128)S(1)} %get-tuple-element.35), channel_id=1, source_target_pairs={{0,1},{1,0},{2,3},{3,2},{4,8},{5,9},{6,10},{7,11},{8,4},{9,5},{10,... | collective-permute-start | bytes 442376 | tf_op jit(solution)/shard_map/ppermute | solution.py:64

commit v2 on v1

--- a/solution.py
+++ b/solution.py
@@ -144,62 +144,150 @@
             o[at : at + plan.corner] = soon[n][pl.ds(base, plan.corner)]
 
 
+class Steps:
+    def __init__(self, plan, levels, pot):
+        self.plan, self.levels, self.pot = plan, levels, pot
+        self.tile = (plan.fields, LANES)
+        lane = lax.broadcasted_iota(jnp.int32, self.tile, 1)
+        masks = ((1, lane >= 1), (LANES - 1, lane < LANES - 1), (2, lane >= 2), (LANES - 2, lane < LANES - 2))
+        self.shifts = masks
+
+    def put_potential(self, first, v, count):
+        scaled = 24.0 * v + 90.0
+        for t in range(count):
+            self.pot[first + t] = jnp.broadcast_to(scaled[t : t + 1, :], self.tile)
+
+    def clear_rows(self, h):
+        plan, i = self.plan, lax.axis_index("gx")
+        for outside, row in ((i == 0, WIDE - 2), (i == plan.gx - 1, WIDE + plan.rows)):
+
+            @pl.when(outside)
+            def _(row=row):
+                for c in range(plan.ext_cols):
+                    at = c * plan.ext_rows + row
+                    h[at : at + 2] = jnp.zeros((2, *self.tile), jnp.float32)
+
+    def clear_cols(self, h):
+        plan, j, long = self.plan, lax.axis_index("gy"), self.plan.ext_rows
+        for outside, col in ((j == 0, WIDE - 2), (j == plan.gy - 1, WIDE + plan.cols)):
+
+            @pl.when(outside)
+            def _(col=col):
+                for c in (col, col + 1):
+                    h[c * long : (c + 1) * long] = jnp.zeros((long, *self.tile), jnp.float32)
+
+    def image(self, h, first, count, use):
+        long = self.plan.ext_rows
+        line = [h[first + t] for t in range(-2, 2)]
+        for t in range(count):
+            at = first + t
+            line.append(h[at + 2])
+            v = line[2]
+            z = [jnp.where(keep, pltpu.roll(v, s, 1), 0.0) for s, keep in self.shifts]
+            near = (line[1] + line[3]) + (h[at - long] + h[at + long]) + (z[0] + z[1])
+            outer = (line[0] + line[4]) + (h[at - 2 * long] + h[at + 2 * long]) + (z[2] + z[3])
+            use(at, t, (outer - 16.0 * near) + self.pot[at] * v)
+            line.pop(0)
+
+    def step(self, k, first, count, spans, unroll):
+        source, target = self.levels[k - 1], self.levels[k]
+
+        def store(at, t, value):
+            target[at] = value
+
+        @pl.loop(0, count, unroll=divisor(count, unroll))
+        def _(t):
+            for row, size in spans:
+                self.image(source, (first(t) if callable(first) else first + t) * self.plan.ext_rows + row, size, store)
+
+    def both_sides(self, inner, m):
+        plan = self.plan
+        if inner:
+            low, high = WIDE + 2 * m - 2, WIDE + plan.cols - 2 * m
+        else:
+            low, high = WIDE - 2 * m, WIDE + plan.cols + 2 * m - 2
+        return lambda t: jnp.where(t < 2, low, high - 2) + t
+
+    def own(self):
+        return [(WIDE, self.plan.rows)]
+
+    def full(self, reach):
+        return [self.plan.span(reach)]
+
+    def outside(self, reach):
+        plan = self.plan
+        return [(plan.beyond(plan.above("gx", kx), reach, plan.rows), reach) for kx in plan.xs] if reach else []
+
+
+def inner_kernel(plan, *refs):
+    nx, ny = len(plan.xs), len(plan.ys)
+    refs = list(refs)
+    take = lambda n: [refs.pop(0) for _ in range(n)]
+    (own,) = take(1)
+    soon, late, big = take(nx), take(nx), take(ny)
+    (v_here,) = take(1)
+    v_there = take(nx)
+    levels, (pot,) = take(ORDER), take(1)
+    rows, cols, long = plan.rows, plan.cols, plan.ext_rows
+    steps = Steps(plan, levels, pot)
+    h0 = levels[0]
+    for c in range(cols):
+        at = (WIDE + c) * long + WIDE
+        h0[at : at + rows] = own[c * rows : (c + 1) * rows]
+        steps.put_potential(at, v_here[c], rows)
+    for n, kx in enumerate(plan.xs):
+        x_hi = plan.above("gx", kx)
+        row, src = plan.beyond(x_hi, WIDE, rows), plan.at_partner(x_hi, WIDE, rows)
+        for c in range(cols):
+            at, size = (WIDE + c) * long + row, plan.soon[c]
+            if size:
+                first = (WIDE + c) * long + plan.beyond(x_hi, size, rows)
+                h0[pl.ds(first, size)] = soon[n][plan.soon_at[c] : plan.soon_at[c + 1]]
+            h0[pl.ds(at + jnp.where(x_hi, size, 0), WIDE - size)] = late[n][plan.late_at[c] : plan.late_at[c + 1]]
+            steps.put_potential(at, v_there[n][c, pl.ds(src, WIDE), :], WIDE)
+    for n, ky in enumerate(plan.ys):
+        base = plan.beyond(plan.above("gy", ky), WIDE, cols)
+        for c in range(WIDE):
+            h0[pl.ds((base + c) * long + WIDE, rows)] = big[n][c * rows : (c + 1) * rows]
+    for h in levels:
+        steps.clear_rows(h)
+    steps.clear_cols(h0)
+    steps.step(1, WIDE + 2, cols - 4, steps.full(6), 4)
+    steps.step(1, steps.both_sides(True, 1), 4, steps.own(), 4)
+    steps.step(2, WIDE + 4, cols - 8, steps.full(4), 4)
+    steps.step(2, steps.both_sides(True, 2), 4, steps.own(), 4)
+    steps.step(3, WIDE + 4, cols - 8, steps.own(), 4)
+
+
 def evolve_kernel(plan, final, *refs):
     nx, ny = len(plan.xs), len(plan.ys)
     refs = list(refs)
     take = lambda n: [refs.pop(0) for _ in range(n)]
-    (own,) = take(1)
-    soon, late, big, edge = take(nx), take(nx), take(ny), take(ny)
-    (v_here,) = take(1)
-    v_there = take(nx)
+    take(ORDER + 1)
+    edge = take(ny)
     if final:
-        orb_ref, v_out = take(2)
+        (v_here,) = take(1)
+    levels, (pot,) = take(ORDER), take(1)
+    if final:
+        orb_ref, v_out, flat = take(3)
     else:
-        (half_ref, dens_ref) = take(2)
+        half_ref, dens_ref = take(2)
         packed = take(ny + 2 * nx)
-    levels = take(ORDER)
-    (pot,) = take(1)
-    if final:
-        (flat,) = take(1)
-    rows, cols, f = plan.rows, plan.cols, plan.fields
-    long = plan.ext_rows
-    i, j = lax.axis_index("gx"), lax.axis_index("gy")
+    rows, cols, f, long = plan.rows, plan.cols, plan.fields, plan.ext_rows
+    steps = Steps(plan, levels, pot)
     h0 = levels[0]
-
-    def put_potential(first, v, count):
-        scaled = 24.0 * v + 90.0
-        for t in range(count):
-            pot[first + t] = jnp.broadcast_to(scaled[t : t + 1, :], (f, LANES))
-
-    for c in range(cols):
-        at = (WIDE + c) * long + WIDE
-        h0[at : at + rows] = own[c * rows : (c + 1) * rows]
-        put_potential(at, v_here[c], rows)
-    for n, kx in enumerate(plan.xs):
-        x_hi = plan.above("gx", kx)
-        row, src = plan.beyond(x_hi, WIDE, rows), plan.at_partner(x_hi, WIDE, rows)
-        for c in range(cols):
-            at = (WIDE + c) * long + row
-            size = plan.soon[c]
-            if size:
-                first = (WIDE + c) * long + plan.beyond(x_hi, size, rows)
-                h0[pl.ds(first, size)] = soon[n][plan.soon_at[c] : plan.soon_at[c + 1]]
-            h0[pl.ds(at + jnp.where(x_hi, size, 0), WIDE - size)] = late[n][plan.late_at[c] : plan.late_at[c + 1]]
-            put_potential(at, v_there[n][c, pl.ds(src, WIDE), :], WIDE)
     for n, ky in enumerate(plan.ys):
         hi = plan.above("gy", ky)
         base = plan.beyond(hi, WIDE, cols)
         for c in range(WIDE):
-            at = (base + c) * long + WIDE
-            h0[pl.ds(at, rows)] = big[n][pl.ds(c * rows, rows)]
-            put_potential(at, edge[n][c], rows)
+            steps.put_potential((base + c) * long + WIDE, edge[n][c], rows)
         for n_x, kx in enumerate(plan.xs):
             at = WIDE + n_x * (plan.v_cols + plan.corner)
             x_hi = plan.above("gx", kx)
             row, src = plan.beyond(x_hi, WIDE, rows), plan.at_partner(x_hi, WIDE, rows)
             first = plan.beyond(hi, plan.v_cols, cols)
             for c in range(plan.v_cols):
-                put_potential((first + c) * long + row, edge[n][at + c, pl.ds(src, WIDE), :], WIDE)
+                steps.put_potential((first + c) * long + row, edge[n][at + c, pl.ds(src, WIDE), :], WIDE)
             at += plan.v_cols
             for d in range(1, WIDE - 1):
                 size = corner_depth(d)
@@ -207,63 +295,26 @@
                 col = jnp.where(hi, WIDE + cols + d - 1, WIDE - d)
                 h0[pl.ds(col * long + plan.beyond(x_hi, size, rows), size)] = edge[n][pl.ds(at + there, size)]
 
-    def clear_outside(h):
-        for outside, col in ((j == 0, WIDE - 2), (j == plan.gy - 1, WIDE + cols)):
-
-            @pl.when(outside)
-            def _(col=col):
-                for c in (col, col + 1):
-                    h[c * long : (c + 1) * long] = jnp.zeros((long, f, LANES), jnp.float32)
-
-        for outside, row in ((i == 0, WIDE - 2), (i == plan.gx - 1, WIDE + rows)):
-
-            @pl.when(outside)
-            def _(row=row):
-                for c in range(plan.ext_cols):
-                    h[c * long + row : c * long + row + 2] = jnp.zeros((2, f, LANES), jnp.float32)
-
-    lane = lax.broadcasted_iota(jnp.int32, (f, LANES), 1)
-    shifts = ((1, lane >= 1), (LANES - 1, lane < LANES - 1), (2, lane >= 2), (LANES - 2, lane < LANES - 2))
-
-    def image(h, first, count, use):
-        line = [h[first + t] for t in range(-2, 2)]
-        for t in range(count):
-            at = first + t
-            line.append(h[at + 2])
-            v = line[2]
-            z = [jnp.where(keep, pltpu.roll(v, s, 1), 0.0) for s, keep in shifts]
-            near = (line[1] + line[3]) + (h[at - long] + h[at + long]) + (z[0] + z[1])
-            outer = (line[0] + line[4]) + (h[at - 2 * long] + h[at + 2 * long]) + (z[2] + z[3])
-            use(at, t, (outer - 16.0 * near) + pot[at] * v)
-            line.pop(0)
-
-    clear_outside(h0)
-    for k in range(1, ORDER):
-        source, target = levels[k - 1], levels[k]
-
-        def column(col, reach, source=source, target=target):
-            row, count = plan.span(reach)
-
-            def store(at, t, value):
-                target[at] = value
-
-            image(source, col * long + row, count, store)
-
-        reach = 2 * (ORDER - k)
-
-        @pl.loop(0, cols, unroll=divisor(cols, 6))
-        def _(c, reach=reach, column=column):
-            column(WIDE + c, reach)
-
-        for m in range(1, ORDER - k + 1):
-            if plan.ys:
-
-                @pl.loop(0, 4, unroll=4)
-                def _(t, m=m, reach=reach, column=column):
-                    col = jnp.where(t < 2, WIDE - 2 * m, WIDE + cols + 2 * m - 4)
-                    column(col + t, reach - 2 * m)
-
-        clear_outside(target)
+    def clear(h):
+        steps.clear_cols(h)
+        if nx > 1:
+            steps.clear_rows(h)
+
+    clear(h0)
+    for m in (1, 2, 3):
+        steps.step(1, steps.both_sides(False, m), 4, steps.full(6 - 2 * m), 4)
+    steps.step(1, steps.both_sides(True, 1), 4, steps.outside(6), 4)
+    clear(levels[1])
+    for m in (1, 2):
+        steps.step(2, steps.both_sides(False, m), 4, steps.full(4 - 2 * m), 4)
+    steps.step(2, steps.both_sides(True, 1), 4, steps.full(4), 4)
+    steps.step(2, steps.both_sides(True, 2), 4, steps.outside(4), 4)
+    clear(levels[2])
+    steps.step(3, steps.both_sides(False, 1), 4, steps.full(0), 4)
+    for m in (1, 2):
+        steps.step(3, steps.both_sides(True, m), 4, steps.full(2), 4)
+    steps.step(3, WIDE + 4, cols - 8, steps.outside(2), 4)
+    clear(levels[3])
 
     sign = jnp.where(lax.broadcasted_iota(jnp.int32, (f, LANES), 0) < plan.bands, 1.0, -1.0)
 
@@ -286,7 +337,7 @@
                 full = total(step_length, g)
                 dens_ref[c, t : t + 1, :] = jnp.sum(full * full, axis=0, keepdims=True)
 
-        image(levels[-1], (WIDE + c) * long + WIDE, rows, finish)
+        steps.image(levels[-1], (WIDE + c) * long + WIDE, rows, finish)
 
     if final:
         v_out[...] = v_here[...]
@@ -299,7 +350,7 @@
         pack(plan, half_ref, packed)
 
 
-def call(kernel, outs, scratch=(), limit=8):
+def call(kernel, outs, scratch=(), limit=8, alias=0):
     spec = pl.BlockSpec(memory_space=pltpu.VMEM)
     return lambda *args: pl.pallas_call(
         kernel,
@@ -307,6 +358,7 @@
         in_specs=[spec] * len(args),
         out_specs=[spec] * len(outs),
         scratch_shapes=list(scratch),
+        input_output_aliases={n: n for n in range(alias)},
         compiler_params=pltpu.CompilerParams(vmem_limit_bytes=limit << 20),
     )(*args)
 
@@ -328,7 +380,14 @@
             [pltpu.VMEM((cells * f, LANES), jnp.float32)],
         )(orbitals)
 
-        def gather(dens, out):
+        extended = (plan.ext_rows * plan.ext_cols, f, LANES)
+
+        def load(ext_ref, out_ref):
+            out_ref[...] = ext_ref[...]
+
+        (external,) = call(load, [plane])(external)
+
+        def gather(fields, dens, out):
             def swap(value, **kinds):
                 return plan.swap(value, **kinds)
 
@@ -343,21 +402,27 @@
                 functools.partial(edge_kernel, plan), [(plan.edge_cells, f, LANES)] * ny
             )(v_here, *v_there, *soon)
             edge = [swap(v, ky=k) for k, v in zip(plan.ys, edge)]
-            return [*soon, *late, *big, *edge, v_here, *v_there]
-
-        extended = pltpu.VMEM((plan.ext_rows * plan.ext_cols, f, LANES), jnp.float32)
-        scratch = [extended] * (ORDER + 1)
-        arrived = gather(dens, out)
+            inside = call(
+                functools.partial(inner_kernel, plan), [extended] * (ORDER + 1), limit=4
+            )(fields, *soon, *late, *big, v_here, *v_there)
+            return [*inside, *edge], v_here
+
+        blocks = [extended] * (ORDER + 1)
+        arrived, _ = gather(fields, dens, out)
         half, dens, *out = call(
-            functools.partial(evolve_kernel, plan, False), [field_shape, plane] + packed, scratch, limit=24
-        )(fields, *arrived)
-        arrived = gather(dens, out)
+            functools.partial(evolve_kernel, plan, False),
+            blocks + [field_shape, plane] + packed,
+            limit=4,
+            alias=len(blocks),
+        )(*arrived)[len(blocks) :]
+        arrived, v_here = gather(half, dens, out)
         result, potential = call(
             functools.partial(evolve_kernel, plan, True),
-            [orbitals.shape, plane],
-            scratch + [pltpu.VMEM((cells * f, LANES), jnp.float32)],
-            limit=24,
-        )(half, *arrived)
+            blocks + [orbitals.shape, plane],
+            [pltpu.VMEM((cells * f, LANES), jnp.float32)],
+            limit=4,
+            alias=len(blocks),
+        )(*arrived, v_here)[len(blocks) :]
         return jnp.swapaxes(result, 2, 3), jnp.swapaxes(potential, 0, 1)
 
     in_specs = (P(None, "band", "gx", "gy", None), P("gx", "gy", None))

time: 48.4 us -> 45.7 us (0.944)
  waiting for transfers between devices: 17.6 us -> 13.4 us
  local copies, waits for them, and re-layouts: 0.99 us -> 1.79 us
  starting transfers between devices: 19.1 us -> 19.9 us
    ppermute x18, waiting for transfers between devices: 17.6 us -> 13.4 us  [swap(): return lax.ppermute(value, AXES, self.pairs(**kinds))]
    unnamed x4, local copies, waits for them, and re-layouts: 0.99 us -> 1.79 us
    ppermute x18, starting transfers between devices: 19.1 us -> 19.9 us  [swap(): return lax.ppermute(value, AXES, self.pairs(**kinds))]
    pallas_call x7 -> x10, Pallas kernels: 9.79 us -> 9.56 us  [call(): pl.pallas_call(kernel, out_shape=[jax.ShapeDtypeStruct(s, jnp.float32) fo...]
  transfers between devices with their start and end apart: 18 -> 18, of which waited for: 7 -> 6; matrix products, arithmetic and copies ran while one was open for 0% -> 0% of each run, Pallas kernels for 0% -> 7%
where the time goes in v2:
time: 45.7 us; the launch traced here: 45.4 us
  starting transfers between devices  19.9 us (44%)
  waiting for transfers between devices  13.4 us (29%)
  Pallas kernels  9.56 us (21%)
  local copies, waits for them, and re-layouts  1.79 us (4%)
  between operations  0.72 us (2%)
    ppermute x18, starting transfers between devices, swap(): return lax.ppermute(value, AXES, self.pairs(**kinds))  19.9 us
    ppermute x18, waiting for transfers between devices, swap(): return lax.ppermute(value, AXES, self.pairs(**kinds))  13.4 us
    pallas_call x10, Pallas kernels, call(): pl.pallas_call(kernel, out_shape=[jax.ShapeDtypeStruct(s, jnp.float32) fo...  9.56 us
    unnamed x4, local copies, waits for them, and re-layouts  1.79 us
  transfers between devices with their start and end apart: 18, of which 6 were waited for; matrix products, arithmetic and copies ran while one was open for 0% of the time, Pallas kernels for 7%

profile of v2, /device:TPU:0, one launch (start us, length us, event | category | flops | bytes accessed | tf_op | source)
XLA Modules:
  0.0 45.4 jit_solution(10215736047088573010)
XLA Ops:
  0.6 1.0 %copy-done = f32[2,4,8,12,128]{4,2,3,1,0:T(8,128)S(1)} copy-done((f32[2,4,8,12,128]{4,2,3,1,0:T(8,128)S(1)}, f32[2,4,8,12,128]{4,2,3,1,0:T(8,128)}, u32[]{:S(2)}) %copy-start) | copy-done | bytes 393240
  1.8 3.0 %collective-permute-start = (f32[48,8,128]{2,1,0:T(8,128)S(1)}, f32[48,8,128]{2,1,0:T(8,128)S(1)}, u32[]{:S(2)}, u32[]{:S(2)}) collective-permute-start(f32[48,8,128]{2,1,0:T(8,128)S(1)} %get-tuple-element.31), channel_id=1, source_target_pairs={{0,16},{1,17},{2,18},{3,19},{4,20},{5,21},{6,22},{7,23},{8,24},{9,... | collective-permute-start | bytes 589832 | tf_op jit(solution)/shard_map/ppermute | solution.py:64
  4.8 1.6 %collective-permute-start.2 = (f32[64,8,128]{2,1,0:T(8,128)S(1)}, f32[64,8,128]{2,1,0:T(8,128)S(1)}, u32[]{:S(2)}, u32[]{:S(2)}) collective-permute-start(f32[64,8,128]{2,1,0:T(8,128)S(1)} %get-tuple-element.33), channel_id=1, source_target_pairs={{0,4},{1,5},{2,6},{3,7},{4,0},{5,1},{6,2},{7,3},{8,12},{9,13},{10,... | collective-permute-start | bytes 786440 | tf_op jit(solution)/shard_map/ppermute | solution.py:64
  6.6 1.6 %collective-permute-start.5 = (f32[12,8,128]{2,1,0:T(8,128)S(1)}, f32[12,8,128]{2,1,0:T(8,128)S(1)}, u32[]{:S(2)}, u32[]{:S(2)}) collective-permute-start(f32[12,8,128]{2,1,0:T(8,128)S(1)} %add.6.refs_0_), channel_id=1, source_target_pairs={{0,2},{1,3},{2,0},{3,1},{4,6},{5,7},{6,4},{7,5},{8,10},{9,11},{10,... | collective-permute-start | bytes 147464 | tf_op jit(solution)/shard_map/ppermute | solution.py:64
  8.2 0.8 %copy-done.1 = f32[8,12,128]{2,0,1:T(8,128)S(1)} copy-done((f32[8,12,128]{2,0,1:T(8,128)S(1)}, f32[8,12,128]{2,0,1:T(8,128)}, u32[]{:S(2)}) %copy-start.1) | copy-done | bytes 49176
  9.0 1.8 %collective-permute-done.5.refs_1_ = f32[12,8,128]{2,1,0:T(8,128)S(1)} collective-permute-done((f32[12,8,128]{2,1,0:T(8,128)S(1)}, f32[12,8,128]{2,1,0:T(8,128)S(1)}, u32[]{:S(2)}, u32[]{:S(2)}) %collective-permute-start.5) | collective-permute-done | bytes 49184 | tf_op jit(solution)/shard_map/ppermute | solution.py:64
  10.8 0.6 %collective-permute-start.6 = (f32[12,8,128]{2,1,0:T(8,128)S(1)}, f32[12,8,128]{2,1,0:T(8,128)S(1)}, u32[]{:S(2)}, u32[]{:S(2)}) collective-permute-start(f32[12,8,128]{2,1,0:T(8,128)S(1)} %shard_map.43.refs_5_.v_here), channel_id=1, source_target_pairs={{0,16},{1,17},{2,18},{3,19},{4,20},{5,21},{6,22},{7,23},{8,24},{9,... | collective-permute-start | bytes 147464 | tf_op jit(solution)/shard_map/ppermute | solution.py:64
  11.4 1.5 %collective-permute-start.1 = (f32[48,8,128]{2,1,0:T(8,128)S(1)}, f32[48,8,128]{2,1,0:T(8,128)S(1)}, u32[]{:S(2)}, u32[]{:S(2)}) collective-permute-start(f32[48,8,128]{2,1,0:T(8,128)S(1)} %get-tuple-element.32), channel_id=1, source_target_pairs={{0,16},{1,17},{2,18},{3,19},{4,20},{5,21},{6,22},{7,23},{8,24},{9,... | collective-permute-start | bytes 589832 | tf_op jit(solution)/shard_map/ppermute | solution.py:64
  12.9 2.6 %collective-permute-done.6.refs_6_.refs_0_ = f32[12,8,128]{2,1,0:T(8,128)S(1)} collective-permute-done((f32[12,8,128]{2,1,0:T(8,128)S(1)}, f32[12,8,128]{2,1,0:T(8,128)S(1)}, u32[]{:S(2)}, u32[]{:S(2)}) %collective-permute-start.6) | collective-permute-done | bytes 49184 | tf_op jit(solution)/shard_map/ppermute | solution.py:64
  15.5 3.0 %collective-permute-start.7 = (f32[36,8,128]{2,1,0:T(8,128)S(1)}, f32[36,8,128]{2,1,0:T(8,128)S(1)}, u32[]{:S(2)}, u32[]{:S(2)}) collective-permute-start(f32[36,8,128]{2,1,0:T(8,128)S(1)} %get-tuple-element.41), channel_id=1, source_target_pairs={{0,4},{1,5},{2,6},{3,7},{4,0},{5,1},{6,2},{7,3},{8,12},{9,13},{10,... | collective-permute-start | bytes 442376 | tf_op jit(solution)/shard_map/ppermute | solution.py:64
  18.6 1.5 %shard_map.44 = (f32[672,8,128]{2,1,0:T(8,128)S(1)}, f32[672,8,128]{2,1,0:T(8,128)S(1)}, f32[672,8,128]{2,1,0:T(8,128)S(1)}, f32[672,8,128]{2,1,0:T(8,128)S(1)}, f32[672,8,128]{2,1,0:T(8,128)S(1)}) custom-call(f32[96,8,128]{2,1,0:T(8,128)S(1)} %get-tuple-element.30.refs_0_, f32[48,8,128]{2,1,0:T(8,128)S(1)} %collective-permute-done.refs_1_, ...), custom_call_target="tpu_custom_call" | custom-call | tf_op jit(solution)/shard_map/pallas_call | solution.py:355
  20.1 1.5 %collective-permute-done.7.refs_5_ = f32[36,8,128]{2,1,0:T(8,128)S(1)} collective-permute-done((f32[36,8,128]{2,1,0:T(8,128)S(1)}, f32[36,8,128]{2,1,0:T(8,128)S(1)}, u32[]{:S(2)}, u32[]{:S(2)}) %collective-permute-start.7) | collective-permute-done | bytes 147488 | tf_op jit(solution)/shard_map/ppermute | solution.py:64
  21.7 2.8 %shard_map.46 = (f32[672,8,128]{2,1,0:T(8,128)S(1)}, f32[672,8,128]{2,1,0:T(8,128)S(1)}, f32[672,8,128]{2,1,0:T(8,128)S(1)}, f32[672,8,128]{2,1,0:T(8,128)S(1)},...) custom-call(f32[672,8,128]{2,1,0:T(8,128)S(1)} %get-tuple-element.36, ...), custom_call_target="tpu_custom_call", output_to_operand_aliasing={{0}: (0, {}), {1}: (1, {}), {2}: (2, {}), {3}: (3, {}), {4}... | custom-call | tf_op jit(solution)/shard_map/pallas_call | solution.py:355
  24.4 0.6 %collective-permute-start.9 = (f32[48,8,128]{2,1,0:T(8,128)S(1)}, f32[48,8,128]{2,1,0:T(8,128)S(1)}, u32[]{:S(2)}, u32[]{:S(2)}) collective-permute-start(f32[48,8,128]{2,1,0:T(8,128)S(1)} %get-tuple-element.44), channel_id=1, source_target_pairs={{0,16},{1,17},{2,18},{3,19},{4,20},{5,21},{6,22},{7,23},{8,24},{9,... | collective-permute-start | bytes 589832 | tf_op jit(solution)/shard_map/ppermute | solution.py:64
  25.0 2.0 %collective-permute-start.11 = (f32[64,8,128]{2,1,0:T(8,128)S(1)}, f32[64,8,128]{2,1,0:T(8,128)S(1)}, u32[]{:S(2)}, u32[]{:S(2)}) collective-permute-start(f32[64,8,128]{2,1,0:T(8,128)S(1)} %get-tuple-element.46), channel_id=1, source_target_pairs={{0,4},{1,5},{2,6},{3,7},{4,0},{5,1},{6,2},{7,3},{8,12},{9,13},{10,... | collective-permute-start | bytes 786440 | tf_op jit(solution)/shard_map/ppermute | solution.py:64
  27.3 1.6 %collective-permute-start.14 = (f32[12,8,128]{2,1,0:T(8,128)S(1)}, f32[12,8,128]{2,1,0:T(8,128)S(1)}, u32[]{:S(2)}, u32[]{:S(2)}) collective-permute-start(f32[12,8,128]{2,1,0:T(8,128)S(1)} %add.7.refs_0_), channel_id=1, source_target_pairs={{0,2},{1,3},{2,0},{3,1},{4,6},{5,7},{6,4},{7,5},{8,10},{9,11},{10,... | collective-permute-start | bytes 147464 | tf_op jit(solution)/shard_map/ppermute | solution.py:64
  28.9 1.5 %collective-permute-start.10 = (f32[48,8,128]{2,1,0:T(8,128)S(1)}, f32[48,8,128]{2,1,0:T(8,128)S(1)}, u32[]{:S(2)}, u32[]{:S(2)}) collective-permute-start(f32[48,8,128]{2,1,0:T(8,128)S(1)} %get-tuple-element.45), channel_id=1, source_target_pairs={{0,16},{1,17},{2,18},{3,19},{4,20},{5,21},{6,22},{7,23},{8,24},{9,... | collective-permute-start | bytes 589832 | tf_op jit(solution)/shard_map/ppermute | solution.py:64
  30.4 1.1 %collective-permute-done.14.refs_1_ = f32[12,8,128]{2,1,0:T(8,128)S(1)} collective-permute-done((f32[12,8,128]{2,1,0:T(8,128)S(1)}, f32[12,8,128]{2,1,0:T(8,128)S(1)}, u32[]{:S(2)}, u32[]{:S(2)}) %collective-permute-start.14) | collective-permute-done | bytes 49184 | tf_op jit(solution)/shard_map/ppermute | solution.py:64
  31.5 1.5 %collective-permute-start.15 = (f32[12,8,128]{2,1,0:T(8,128)S(1)}, f32[12,8,128]{2,1,0:T(8,128)S(1)}, u32[]{:S(2)}, u32[]{:S(2)}) collective-permute-start(f32[12,8,128]{2,1,0:T(8,128)S(1)} %shard_map.47.refs_5_.v_here.refs_7_), channel_id=1, source_target_pairs={{0,16},{1,17},{2,18},{3,19},{4,20},{5,21},{6,22},{7,23},{8,24},{9,... | collective-permute-start | bytes 147464 | tf_op jit(solution)/shard_map/ppermute | solution.py:64
  33.1 3.7 %collective-permute-done.15.refs_6_.refs_0_ = f32[12,8,128]{2,1,0:T(8,128)S(1)} collective-permute-done((f32[12,8,128]{2,1,0:T(8,128)S(1)}, f32[12,8,128]{2,1,0:T(8,128)S(1)}, u32[]{:S(2)}, u32[]{:S(2)}) %collective-permute-start.15) | collective-permute-done | bytes 49184 | tf_op jit(solution)/shard_map/ppermute | solution.py:64
  36.8 0.9 %collective-permute-start.16 = (f32[36,8,128]{2,1,0:T(8,128)S(1)}, f32[36,8,128]{2,1,0:T(8,128)S(1)}, u32[]{:S(2)}, u32[]{:S(2)}) collective-permute-start(f32[36,8,128]{2,1,0:T(8,128)S(1)} %get-tuple-element.54), channel_id=1, source_target_pairs={{0,4},{1,5},{2,6},{3,7},{4,0},{5,1},{6,2},{7,3},{8,12},{9,13},{10,... | collective-permute-start | bytes 442376 | tf_op jit(solution)/shard_map/ppermute | solution.py:64
  37.7 1.5 %shard_map.48 = (f32[672,8,128]{2,1,0:T(8,128)S(1)}, f32[672,8,128]{2,1,0:T(8,128)S(1)}, f32[672,8,128]{2,1,0:T(8,128)S(1)}, f32[672,8,128]{2,1,0:T(8,128)S(1)}, f32[672,8,128]{2,1,0:T(8,128)S(1)}) custom-call(f32[96,8,128]{2,1,0:T(8,128)S(1)} %get-tuple-element.43.refs_0_, f32[48,8,128]{2,1,0:T(8,128)S(1)} %collective-permute-done.9.refs_1_, ...), custom_call_target="tpu_custom_call" | custom-call | tf_op jit(solution)/shard_map/pallas_call | solution.py:355
  39.3 2.7 %collective-permute-done.16.refs_5_ = f32[36,8,128]{2,1,0:T(8,128)S(1)} collective-permute-done((f32[36,8,128]{2,1,0:T(8,128)S(1)}, f32[36,8,128]{2,1,0:T(8,128)S(1)}, u32[]{:S(2)}, u32[]{:S(2)}) %collective-permute-start.16) | collective-permute-done | bytes 147488 | tf_op jit(solution)/shard_map/ppermute | solution.py:64
  42.0 3.4 %shard_map.50 = (f32[672,8,128]{2,1,0:T(8,128)S(1)}, f32[672,8,128]{2,1,0:T(8,128)S(1)}, f32[672,8,128]{2,1,0:T(8,128)S(1)}, f32[672,8,128]{2,1,0:T(8,128)S(1)},...) custom-call(f32[672,8,128]{2,1,0:T(8,128)S(1)} %get-tuple-element.49, ...), custom_call_target="tpu_custom_call", output_to_operand_aliasing={{0}: (0, {}), {1}: (1, {}), {2}: (2, {}), {3}: (3, {}), {4}... | custom-call | tf_op jit(solution)/shard_map/pallas_call | solution.py:355
  (28 shorter events, 0.8 us)
Async XLA Ops:
  0.6 1.0 %copy-start = (f32[2,4,8,12,128]{4,2,3,1,0:T(8,128)S(1)}, f32[2,4,8,12,128]{4,2,3,1,0:T(8,128)}, u32[]{:S(2)}) copy-start(f32[2,4,8,12,128]{4,2,3,1,0:T(8,128)} %param.2) | copy-start | bytes 1179652
  1.8 13.7 %collective-permute-start = (f32[48,8,128]{2,1,0:T(8,128)S(1)}, f32[48,8,128]{2,1,0:T(8,128)S(1)}, u32[]{:S(2)}, u32[]{:S(2)}) collective-permute-start(f32[48,8,128]{2,1,0:T(8,128)S(1)} %get-tuple-element.31), channel_id=1, source_target_pairs={{0,16},{1,17},{2,18},{3,19},{4,20},{5,21},{6,22},{7,23},{8,24},{9,... | collective-permute-start | bytes 589832 | tf_op jit(solution)/shard_map/ppermute | solution.py:64
  4.8 1.8 %collective-permute-start.4 = (f32[12,8,128]{2,1,0:T(8,128)S(1)}, f32[12,8,128]{2,1,0:T(8,128)S(1)}, u32[]{:S(2)}, u32[]{:S(2)}) collective-permute-start(f32[12,8,128]{2,1,0:T(8,128)S(1)} %get-tuple-element.35), channel_id=1, source_target_pairs={{0,1},{1,0},{2,3},{3,2},{4,5},{5,4},{6,7},{7,6},{8,9},{9,8},{10,11... | collective-permute-start | bytes 147464 | tf_op jit(solution)/shard_map/ppermute | solution.py:64
  4.8 13.7 %collective-permute-start.2 = (f32[64,8,128]{2,1,0:T(8,128)S(1)}, f32[64,8,128]{2,1,0:T(8,128)S(1)}, u32[]{:S(2)}, u32[]{:S(2)}) collective-permute-start(f32[64,8,128]{2,1,0:T(8,128)S(1)} %get-tuple-element.33), channel_id=1, source_target_pairs={{0,4},{1,5},{2,6},{3,7},{4,0},{5,1},{6,2},{7,3},{8,12},{9,13},{10,... | collective-permute-start | bytes 786440 | tf_op jit(solution)/shard_map/ppermute | solution.py:64
  6.4 12.2 %collective-permute-start.3 = (f32[64,8,128]{2,1,0:T(8,128)S(1)}, f32[64,8,128]{2,1,0:T(8,128)S(1)}, u32[]{:S(2)}, u32[]{:S(2)}) collective-permute-start(f32[64,8,128]{2,1,0:T(8,128)S(1)} %get-tuple-element.34), channel_id=1, source_target_pairs={{0,1},{1,0},{2,3},{3,2},{4,8},{5,9},{6,10},{7,11},{8,4},{9,5},{10,... | collective-permute-start | bytes 786440 | tf_op jit(solution)/shard_map/ppermute | solution.py:64
  6.6 4.2 %collective-permute-start.5 = (f32[12,8,128]{2,1,0:T(8,128)S(1)}, f32[12,8,128]{2,1,0:T(8,128)S(1)}, u32[]{:S(2)}, u32[]{:S(2)}) collective-permute-start(f32[12,8,128]{2,1,0:T(8,128)S(1)} %add.6.refs_0_), channel_id=1, source_target_pairs={{0,2},{1,3},{2,0},{3,1},{4,6},{5,7},{6,4},{7,5},{8,10},{9,11},{10,... | collective-permute-start | bytes 147464 | tf_op jit(solution)/shard_map/ppermute | solution.py:64
  8.2 0.8 %copy-start.1 = (f32[8,12,128]{2,0,1:T(8,128)S(1)}, f32[8,12,128]{2,0,1:T(8,128)}, u32[]{:S(2)}) copy-start(f32[8,12,128]{2,0,1:T(8,128)} %param.3) | copy-start | bytes 147460
  10.8 4.7 %collective-permute-start.6 = (f32[12,8,128]{2,1,0:T(8,128)S(1)}, f32[12,8,128]{2,1,0:T(8,128)S(1)}, u32[]{:S(2)}, u32[]{:S(2)}) collective-permute-start(f32[12,8,128]{2,1,0:T(8,128)S(1)} %shard_map.43.refs_5_.v_here), channel_id=1, source_target_pairs={{0,16},{1,17},{2,18},{3,19},{4,20},{5,21},{6,22},{7,23},{8,24},{9,... | collective-permute-start | bytes 147464 | tf_op jit(solution)/shard_map/ppermute | solution.py:64
  11.4 7.1 %collective-permute-start.1 = (f32[48,8,128]{2,1,0:T(8,128)S(1)}, f32[48,8,128]{2,1,0:T(8,128)S(1)}, u32[]{:S(2)}, u32[]{:S(2)}) collective-permute-start(f32[48,8,128]{2,1,0:T(8,128)S(1)} %get-tuple-element.32), channel_id=1, source_target_pairs={{0,16},{1,17},{2,18},{3,19},{4,20},{5,21},{6,22},{7,23},{8,24},{9,... | collective-permute-start | bytes 589832 | tf_op jit(solution)/shard_map/ppermute | solution.py:64
  15.5 6.1 %collective-permute-start.7 = (f32[36,8,128]{2,1,0:T(8,128)S(1)}, f32[36,8,128]{2,1,0:T(8,128)S(1)}, u32[]{:S(2)}, u32[]{:S(2)}) collective-permute-start(f32[36,8,128]{2,1,0:T(8,128)S(1)} %get-tuple-element.41), channel_id=1, source_target_pairs={{0,4},{1,5},{2,6},{3,7},{4,0},{5,1},{6,2},{7,3},{8,12},{9,13},{10,... | collective-permute-start | bytes 442376 | tf_op jit(solution)/shard_map/ppermute | solution.py:64
  18.5 3.1 %collective-permute-start.8 = (f32[36,8,128]{2,1,0:T(8,128)S(1)}, f32[36,8,128]{2,1,0:T(8,128)S(1)}, u32[]{:S(2)}, u32[]{:S(2)}) collective-permute-start(f32[36,8,128]{2,1,0:T(8,128)S(1)} %get-tuple-element.42), channel_id=1, source_target_pairs={{0,1},{1,0},{2,3},{3,2},{4,8},{5,9},{6,10},{7,11},{8,4},{9,5},{10,... | collective-permute-start | bytes 442376 | tf_op jit(solution)/shard_map/ppermute | solution.py:64
  24.4 12.3 %collective-permute-start.9 = (f32[48,8,128]{2,1,0:T(8,128)S(1)}, f32[48,8,128]{2,1,0:T(8,128)S(1)}, u32[]{:S(2)}, u32[]{:S(2)}) collective-permute-start(f32[48,8,128]{2,1,0:T(8,128)S(1)} %get-tuple-element.44), channel_id=1, source_target_pairs={{0,16},{1,17},{2,18},{3,19},{4,20},{5,21},{6,22},{7,23},{8,24},{9,... | collective-permute-start | bytes 589832 | tf_op jit(solution)/shard_map/ppermute | solution.py:64
  25.0 2.3 %collective-permute-start.13 = (f32[12,8,128]{2,1,0:T(8,128)S(1)}, f32[12,8,128]{2,1,0:T(8,128)S(1)}, u32[]{:S(2)}, u32[]{:S(2)}) collective-permute-start(f32[12,8,128]{2,1,0:T(8,128)S(1)} %get-tuple-element.48), channel_id=1, source_target_pairs={{0,1},{1,0},{2,3},{3,2},{4,5},{5,4},{6,7},{7,6},{8,9},{9,8},{10,11... | collective-permute-start | bytes 147464 | tf_op jit(solution)/shard_map/ppermute | solution.py:64
  25.0 12.7 %collective-permute-start.11 = (f32[64,8,128]{2,1,0:T(8,128)S(1)}, f32[64,8,128]{2,1,0:T(8,128)S(1)}, u32[]{:S(2)}, u32[]{:S(2)}) collective-permute-start(f32[64,8,128]{2,1,0:T(8,128)S(1)} %get-tuple-element.46), channel_id=1, source_target_pairs={{0,4},{1,5},{2,6},{3,7},{4,0},{5,1},{6,2},{7,3},{8,12},{9,13},{10,... | collective-permute-start | bytes 786440 | tf_op jit(solution)/shard_map/ppermute | solution.py:64
  27.1 10.7 %collective-permute-start.12 = (f32[64,8,128]{2,1,0:T(8,128)S(1)}, f32[64,8,128]{2,1,0:T(8,128)S(1)}, u32[]{:S(2)}, u32[]{:S(2)}) collective-permute-start(f32[64,8,128]{2,1,0:T(8,128)S(1)} %get-tuple-element.47), channel_id=1, source_target_pairs={{0,1},{1,0},{2,3},{3,2},{4,8},{5,9},{6,10},{7,11},{8,4},{9,5},{10,... | collective-permute-start | bytes 786440 | tf_op jit(solution)/shard_map/ppermute | solution.py:64
  27.3 4.2 %collective-permute-start.14 = (f32[12,8,128]{2,1,0:T(8,128)S(1)}, f32[12,8,128]{2,1,0:T(8,128)S(1)}, u32[]{:S(2)}, u32[]{:S(2)}) collective-permute-start(f32[12,8,128]{2,1,0:T(8,128)S(1)} %add.7.refs_0_), channel_id=1, source_target_pairs={{0,2},{1,3},{2,0},{3,1},{4,6},{5,7},{6,4},{7,5},{8,10},{9,11},{10,... | collective-permute-start | bytes 147464 | tf_op jit(solution)/shard_map/ppermute | solution.py:64
  28.9 8.8 %collective-permute-start.10 = (f32[48,8,128]{2,1,0:T(8,128)S(1)}, f32[48,8,128]{2,1,0:T(8,128)S(1)}, u32[]{:S(2)}, u32[]{:S(2)}) collective-permute-start(f32[48,8,128]{2,1,0:T(8,128)S(1)} %get-tuple-element.45), channel_id=1, source_target_pairs={{0,16},{1,17},{2,18},{3,19},{4,20},{5,21},{6,22},{7,23},{8,24},{9,... | collective-permute-start | bytes 589832 | tf_op jit(solution)/shard_map/ppermute | solution.py:64
  31.5 5.2 %collective-permute-start.15 = (f32[12,8,128]{2,1,0:T(8,128)S(1)}, f32[12,8,128]{2,1,0:T(8,128)S(1)}, u32[]{:S(2)}, u32[]{:S(2)}) collective-permute-start(f32[12,8,128]{2,1,0:T(8,128)S(1)} %shard_map.47.refs_5_.v_here.refs_7_), channel_id=1, source_target_pairs={{0,16},{1,17},{2,18},{3,19},{4,20},{5,21},{6,22},{7,23},{8,24},{9,... | collective-permute-start | bytes 147464 | tf_op jit(solution)/shard_map/ppermute | solution.py:64
  36.8 5.2 %collective-permute-start.16 = (f32[36,8,128]{2,1,0:T(8,128)S(1)}, f32[36,8,128]{2,1,0:T(8,128)S(1)}, u32[]{:S(2)}, u32[]{:S(2)}) collective-permute-start(f32[36,8,128]{2,1,0:T(8,128)S(1)} %get-tuple-element.54), channel_id=1, source_target_pairs={{0,4},{1,5},{2,6},{3,7},{4,0},{5,1},{6,2},{7,3},{8,12},{9,13},{10,... | collective-permute-start | bytes 442376 | tf_op jit(solution)/shard_map/ppermute | solution.py:64
  37.7 4.3 %collective-permute-start.17 = (f32[36,8,128]{2,1,0:T(8,128)S(1)}, f32[36,8,128]{2,1,0:T(8,128)S(1)}, u32[]{:S(2)}, u32[]{:S(2)}) collective-permute-start(f32[36,8,128]{2,1,0:T(8,128)S(1)} %get-tuple-element.55), channel_id=1, source_target_pairs={{0,1},{1,0},{2,3},{3,2},{4,8},{5,9},{6,10},{7,11},{8,4},{9,5},{10,... | collective-permute-start | bytes 442376 | tf_op jit(solution)/shard_map/ppermute | solution.py:64

commit v3 on v2

--- a/solution.py
+++ b/solution.py
@@ -148,9 +148,17 @@
     def __init__(self, plan, levels, pot):
         self.plan, self.levels, self.pot = plan, levels, pot
         self.tile = (plan.fields, LANES)
-        lane = lax.broadcasted_iota(jnp.int32, self.tile, 1)
-        masks = ((1, lane >= 1), (LANES - 1, lane < LANES - 1), (2, lane >= 2), (LANES - 2, lane < LANES - 2))
-        self.shifts = masks
+        apart = lax.broadcasted_iota(jnp.int32, (LANES, LANES), 0) - lax.broadcasted_iota(jnp.int32, (LANES, LANES), 1)
+        apart = jnp.abs(apart)
+        weights = jnp.where(apart == 1, -16.0, jnp.where(apart == 2, 1.0, 0.0))
+        self.weights = weights.astype(jnp.bfloat16)
+
+    def along_z(self, cells):
+        flat = cells.reshape(-1, LANES)
+        high = flat.astype(jnp.bfloat16)
+        low = (flat - high.astype(jnp.float32)).astype(jnp.bfloat16)
+        times = lambda v: jnp.dot(v, self.weights, preferred_element_type=jnp.float32)
+        return (times(high) + times(low)).reshape(cells.shape)
 
     def put_potential(self, first, v, count):
         scaled = 24.0 * v + 90.0
@@ -179,14 +187,14 @@
     def image(self, h, first, count, use):
         long = self.plan.ext_rows
         line = [h[first + t] for t in range(-2, 2)]
+        z = self.along_z(h[pl.ds(first, count)])
         for t in range(count):
             at = first + t
             line.append(h[at + 2])
             v = line[2]
-            z = [jnp.where(keep, pltpu.roll(v, s, 1), 0.0) for s, keep in self.shifts]
-            near = (line[1] + line[3]) + (h[at - long] + h[at + long]) + (z[0] + z[1])
-            outer = (line[0] + line[4]) + (h[at - 2 * long] + h[at + 2 * long]) + (z[2] + z[3])
-            use(at, t, (outer - 16.0 * near) + self.pot[at] * v)
+            near = (line[1] + line[3]) + (h[at - long] + h[at + long])
+            outer = (line[0] + line[4]) + (h[at - 2 * long] + h[at + 2 * long])
+            use(at, t, (outer - 16.0 * near) + (z[t] + self.pot[at] * v))
             line.pop(0)
 
     def step(self, k, first, count, spans, unroll):

time: 45.7 us -> 44.6 us (0.976)
  Pallas kernels: 9.56 us -> 7.95 us
  waiting for transfers between devices: 13.4 us -> 14 us
    pallas_call x10, Pallas kernels: 9.56 us -> 7.95 us  [call(): pl.pallas_call(kernel, out_shape=[jax.ShapeDtypeStruct(s, jnp.float32) fo...]
    ppermute x18, waiting for transfers between devices: 13.4 us -> 14 us  [swap(): return lax.ppermute(value, AXES, self.pairs(**kinds))]
  transfers between devices with their start and end apart: 18 -> 18, of which waited for: 6 -> 6; matrix products, arithmetic and copies ran while one was open for 0% -> 0% of each run, Pallas kernels for 7% -> 6%
where the time goes in v3:
time: 44.6 us; the launch traced here: 44.4 us
  starting transfers between devices  19.9 us (45%)
  waiting for transfers between devices  14 us (31%)
  Pallas kernels  7.95 us (18%)
  local copies, waits for them, and re-layouts  1.79 us (4%)
  between operations  0.72 us (2%)
    ppermute x18, starting transfers between devices, swap(): return lax.ppermute(value, AXES, self.pairs(**kinds))  19.9 us
    ppermute x18, waiting for transfers between devices, swap(): return lax.ppermute(value, AXES, self.pairs(**kinds))  14 us
    pallas_call x10, Pallas kernels, call(): pl.pallas_call(kernel, out_shape=[jax.ShapeDtypeStruct(s, jnp.float32) fo...  7.95 us
    unnamed x4, local copies, waits for them, and re-layouts  1.79 us
  transfers between devices with their start and end apart: 18, of which 6 were waited for; matrix products, arithmetic and copies ran while one was open for 0% of the time, Pallas kernels for 6%

profile of v3, /device:TPU:0, one launch (start us, length us, event | category | flops | bytes accessed | tf_op | source)
XLA Modules:
  0.0 44.4 jit_solution(14853090970352924696)
XLA Ops:
  0.6 1.0 %copy-done = f32[2,4,8,12,128]{4,2,3,1,0:T(8,128)S(1)} copy-done((f32[2,4,8,12,128]{4,2,3,1,0:T(8,128)S(1)}, f32[2,4,8,12,128]{4,2,3,1,0:T(8,128)}, u32[]{:S(2)}) %copy-start) | copy-done | bytes 393240
  1.8 3.0 %collective-permute-start = (f32[48,8,128]{2,1,0:T(8,128)S(1)}, f32[48,8,128]{2,1,0:T(8,128)S(1)}, u32[]{:S(2)}, u32[]{:S(2)}) collective-permute-start(f32[48,8,128]{2,1,0:T(8,128)S(1)} %get-tuple-element.31), channel_id=1, source_target_pairs={{0,16},{1,17},{2,18},{3,19},{4,20},{5,21},{6,22},{7,23},{8,24},{9,... | collective-permute-start | bytes 589832 | tf_op jit(solution)/shard_map/ppermute | solution.py:64
  4.8 1.6 %collective-permute-start.2 = (f32[64,8,128]{2,1,0:T(8,128)S(1)}, f32[64,8,128]{2,1,0:T(8,128)S(1)}, u32[]{:S(2)}, u32[]{:S(2)}) collective-permute-start(f32[64,8,128]{2,1,0:T(8,128)S(1)} %get-tuple-element.33), channel_id=1, source_target_pairs={{0,4},{1,5},{2,6},{3,7},{4,0},{5,1},{6,2},{7,3},{8,12},{9,13},{10,... | collective-permute-start | bytes 786440 | tf_op jit(solution)/shard_map/ppermute | solution.py:64
  6.6 1.6 %collective-permute-start.5 = (f32[12,8,128]{2,1,0:T(8,128)S(1)}, f32[12,8,128]{2,1,0:T(8,128)S(1)}, u32[]{:S(2)}, u32[]{:S(2)}) collective-permute-start(f32[12,8,128]{2,1,0:T(8,128)S(1)} %add.6.refs_0_), channel_id=1, source_target_pairs={{0,2},{1,3},{2,0},{3,1},{4,6},{5,7},{6,4},{7,5},{8,10},{9,11},{10,... | collective-permute-start | bytes 147464 | tf_op jit(solution)/shard_map/ppermute | solution.py:64
  8.2 0.8 %copy-done.1 = f32[8,12,128]{2,0,1:T(8,128)S(1)} copy-done((f32[8,12,128]{2,0,1:T(8,128)S(1)}, f32[8,12,128]{2,0,1:T(8,128)}, u32[]{:S(2)}) %copy-start.1) | copy-done | bytes 49176
  9.0 1.8 %collective-permute-done.5.refs_1_ = f32[12,8,128]{2,1,0:T(8,128)S(1)} collective-permute-done((f32[12,8,128]{2,1,0:T(8,128)S(1)}, f32[12,8,128]{2,1,0:T(8,128)S(1)}, u32[]{:S(2)}, u32[]{:S(2)}) %collective-permute-start.5) | collective-permute-done | bytes 49184 | tf_op jit(solution)/shard_map/ppermute | solution.py:64
  10.8 0.6 %collective-permute-start.6 = (f32[12,8,128]{2,1,0:T(8,128)S(1)}, f32[12,8,128]{2,1,0:T(8,128)S(1)}, u32[]{:S(2)}, u32[]{:S(2)}) collective-permute-start(f32[12,8,128]{2,1,0:T(8,128)S(1)} %shard_map.43.refs_5_.v_here), channel_id=1, source_target_pairs={{0,16},{1,17},{2,18},{3,19},{4,20},{5,21},{6,22},{7,23},{8,24},{9,... | collective-permute-start | bytes 147464 | tf_op jit(solution)/shard_map/ppermute | solution.py:64
  11.4 1.5 %collective-permute-start.1 = (f32[48,8,128]{2,1,0:T(8,128)S(1)}, f32[48,8,128]{2,1,0:T(8,128)S(1)}, u32[]{:S(2)}, u32[]{:S(2)}) collective-permute-start(f32[48,8,128]{2,1,0:T(8,128)S(1)} %get-tuple-element.32), channel_id=1, source_target_pairs={{0,16},{1,17},{2,18},{3,19},{4,20},{5,21},{6,22},{7,23},{8,24},{9,... | collective-permute-start | bytes 589832 | tf_op jit(solution)/shard_map/ppermute | solution.py:64
  12.9 2.6 %collective-permute-done.6.refs_6_.refs_0_ = f32[12,8,128]{2,1,0:T(8,128)S(1)} collective-permute-done((f32[12,8,128]{2,1,0:T(8,128)S(1)}, f32[12,8,128]{2,1,0:T(8,128)S(1)}, u32[]{:S(2)}, u32[]{:S(2)}) %collective-permute-start.6) | collective-permute-done | bytes 49184 | tf_op jit(solution)/shard_map/ppermute | solution.py:64
  15.5 3.0 %collective-permute-start.7 = (f32[36,8,128]{2,1,0:T(8,128)S(1)}, f32[36,8,128]{2,1,0:T(8,128)S(1)}, u32[]{:S(2)}, u32[]{:S(2)}) collective-permute-start(f32[36,8,128]{2,1,0:T(8,128)S(1)} %get-tuple-element.41), channel_id=1, source_target_pairs={{0,4},{1,5},{2,6},{3,7},{4,0},{5,1},{6,2},{7,3},{8,12},{9,13},{10,... | collective-permute-start | bytes 442376 | tf_op jit(solution)/shard_map/ppermute | solution.py:64
  18.6 1.3 %shard_map.44 = (f32[672,8,128]{2,1,0:T(8,128)S(1)}, f32[672,8,128]{2,1,0:T(8,128)S(1)}, f32[672,8,128]{2,1,0:T(8,128)S(1)}, f32[672,8,128]{2,1,0:T(8,128)S(1)}, f32[672,8,128]{2,1,0:T(8,128)S(1)}) custom-call(f32[96,8,128]{2,1,0:T(8,128)S(1)} %get-tuple-element.30.refs_0_, f32[48,8,128]{2,1,0:T(8,128)S(1)} %collective-permute-done.refs_1_, ...), custom_call_target="tpu_custom_call" | custom-call | tf_op jit(solution)/shard_map/pallas_call | solution.py:363
  19.9 1.8 %collective-permute-done.7.refs_5_ = f32[36,8,128]{2,1,0:T(8,128)S(1)} collective-permute-done((f32[36,8,128]{2,1,0:T(8,128)S(1)}, f32[36,8,128]{2,1,0:T(8,128)S(1)}, u32[]{:S(2)}, u32[]{:S(2)}) %collective-permute-start.7) | collective-permute-done | bytes 147488 | tf_op jit(solution)/shard_map/ppermute | solution.py:64
  21.7 2.3 %shard_map.46 = (f32[672,8,128]{2,1,0:T(8,128)S(1)}, f32[672,8,128]{2,1,0:T(8,128)S(1)}, f32[672,8,128]{2,1,0:T(8,128)S(1)}, f32[672,8,128]{2,1,0:T(8,128)S(1)},...) custom-call(f32[672,8,128]{2,1,0:T(8,128)S(1)} %get-tuple-element.36, ...), custom_call_target="tpu_custom_call", output_to_operand_aliasing={{0}: (0, {}), {1}: (1, {}), {2}: (2, {}), {3}: (3, {}), {4}... | custom-call | tf_op jit(solution)/shard_map/pallas_call | solution.py:363
  23.9 0.7 %collective-permute-start.9 = (f32[48,8,128]{2,1,0:T(8,128)S(1)}, f32[48,8,128]{2,1,0:T(8,128)S(1)}, u32[]{:S(2)}, u32[]{:S(2)}) collective-permute-start(f32[48,8,128]{2,1,0:T(8,128)S(1)} %get-tuple-element.44), channel_id=1, source_target_pairs={{0,16},{1,17},{2,18},{3,19},{4,20},{5,21},{6,22},{7,23},{8,24},{9,... | collective-permute-start | bytes 589832 | tf_op jit(solution)/shard_map/ppermute | solution.py:64
  24.6 2.0 %collective-permute-start.11 = (f32[64,8,128]{2,1,0:T(8,128)S(1)}, f32[64,8,128]{2,1,0:T(8,128)S(1)}, u32[]{:S(2)}, u32[]{:S(2)}) collective-permute-start(f32[64,8,128]{2,1,0:T(8,128)S(1)} %get-tuple-element.46), channel_id=1, source_target_pairs={{0,4},{1,5},{2,6},{3,7},{4,0},{5,1},{6,2},{7,3},{8,12},{9,13},{10,... | collective-permute-start | bytes 786440 | tf_op jit(solution)/shard_map/ppermute | solution.py:64
  26.9 1.6 %collective-permute-start.14 = (f32[12,8,128]{2,1,0:T(8,128)S(1)}, f32[12,8,128]{2,1,0:T(8,128)S(1)}, u32[]{:S(2)}, u32[]{:S(2)}) collective-permute-start(f32[12,8,128]{2,1,0:T(8,128)S(1)} %add.7.refs_0_), channel_id=1, source_target_pairs={{0,2},{1,3},{2,0},{3,1},{4,6},{5,7},{6,4},{7,5},{8,10},{9,11},{10,... | collective-permute-start | bytes 147464 | tf_op jit(solution)/shard_map/ppermute | solution.py:64
  28.4 1.5 %collective-permute-start.10 = (f32[48,8,128]{2,1,0:T(8,128)S(1)}, f32[48,8,128]{2,1,0:T(8,128)S(1)}, u32[]{:S(2)}, u32[]{:S(2)}) collective-permute-start(f32[48,8,128]{2,1,0:T(8,128)S(1)} %get-tuple-element.45), channel_id=1, source_target_pairs={{0,16},{1,17},{2,18},{3,19},{4,20},{5,21},{6,22},{7,23},{8,24},{9,... | collective-permute-start | bytes 589832 | tf_op jit(solution)/shard_map/ppermute | solution.py:64
  29.9 1.1 %collective-permute-done.14.refs_1_ = f32[12,8,128]{2,1,0:T(8,128)S(1)} collective-permute-done((f32[12,8,128]{2,1,0:T(8,128)S(1)}, f32[12,8,128]{2,1,0:T(8,128)S(1)}, u32[]{:S(2)}, u32[]{:S(2)}) %collective-permute-start.14) | collective-permute-done | bytes 49184 | tf_op jit(solution)/shard_map/ppermute | solution.py:64
  31.1 1.5 %collective-permute-start.15 = (f32[12,8,128]{2,1,0:T(8,128)S(1)}, f32[12,8,128]{2,1,0:T(8,128)S(1)}, u32[]{:S(2)}, u32[]{:S(2)}) collective-permute-start(f32[12,8,128]{2,1,0:T(8,128)S(1)} %shard_map.47.refs_5_.v_here.refs_7_), channel_id=1, source_target_pairs={{0,16},{1,17},{2,18},{3,19},{4,20},{5,21},{6,22},{7,23},{8,24},{9,... | collective-permute-start | bytes 147464 | tf_op jit(solution)/shard_map/ppermute | solution.py:64
  32.6 3.7 %collective-permute-done.15.refs_6_.refs_0_ = f32[12,8,128]{2,1,0:T(8,128)S(1)} collective-permute-done((f32[12,8,128]{2,1,0:T(8,128)S(1)}, f32[12,8,128]{2,1,0:T(8,128)S(1)}, u32[]{:S(2)}, u32[]{:S(2)}) %collective-permute-start.15) | collective-permute-done | bytes 49184 | tf_op jit(solution)/shard_map/ppermute | solution.py:64
  36.3 0.9 %collective-permute-start.16 = (f32[36,8,128]{2,1,0:T(8,128)S(1)}, f32[36,8,128]{2,1,0:T(8,128)S(1)}, u32[]{:S(2)}, u32[]{:S(2)}) collective-permute-start(f32[36,8,128]{2,1,0:T(8,128)S(1)} %get-tuple-element.54), channel_id=1, source_target_pairs={{0,4},{1,5},{2,6},{3,7},{4,0},{5,1},{6,2},{7,3},{8,12},{9,13},{10,... | collective-permute-start | bytes 442376 | tf_op jit(solution)/shard_map/ppermute | solution.py:64
  37.3 1.3 %shard_map.48 = (f32[672,8,128]{2,1,0:T(8,128)S(1)}, f32[672,8,128]{2,1,0:T(8,128)S(1)}, f32[672,8,128]{2,1,0:T(8,128)S(1)}, f32[672,8,128]{2,1,0:T(8,128)S(1)}, f32[672,8,128]{2,1,0:T(8,128)S(1)}) custom-call(f32[96,8,128]{2,1,0:T(8,128)S(1)} %get-tuple-element.43.refs_0_, f32[48,8,128]{2,1,0:T(8,128)S(1)} %collective-permute-done.9.refs_1_, ...), custom_call_target="tpu_custom_call" | custom-call | tf_op jit(solution)/shard_map/pallas_call | solution.py:363
  38.6 3.0 %collective-permute-done.16.refs_5_ = f32[36,8,128]{2,1,0:T(8,128)S(1)} collective-permute-done((f32[36,8,128]{2,1,0:T(8,128)S(1)}, f32[36,8,128]{2,1,0:T(8,128)S(1)}, u32[]{:S(2)}, u32[]{:S(2)}) %collective-permute-start.16) | collective-permute-done | bytes 147488 | tf_op jit(solution)/shard_map/ppermute | solution.py:64
  41.5 2.8 %shard_map.50 = (f32[672,8,128]{2,1,0:T(8,128)S(1)}, f32[672,8,128]{2,1,0:T(8,128)S(1)}, f32[672,8,128]{2,1,0:T(8,128)S(1)}, f32[672,8,128]{2,1,0:T(8,128)S(1)},...) custom-call(f32[672,8,128]{2,1,0:T(8,128)S(1)} %get-tuple-element.49, ...), custom_call_target="tpu_custom_call", output_to_operand_aliasing={{0}: (0, {}), {1}: (1, {}), {2}: (2, {}), {3}: (3, {}), {4}... | custom-call | tf_op jit(solution)/shard_map/pallas_call | solution.py:363
  (28 shorter events, 0.8 us)
Async XLA Ops:
  0.6 1.0 %copy-start = (f32[2,4,8,12,128]{4,2,3,1,0:T(8,128)S(1)}, f32[2,4,8,12,128]{4,2,3,1,0:T(8,128)}, u32[]{:S(2)}) copy-start(f32[2,4,8,12,128]{4,2,3,1,0:T(8,128)} %param.2) | copy-start | bytes 1179652
  1.8 13.7 %collective-permute-start = (f32[48,8,128]{2,1,0:T(8,128)S(1)}, f32[48,8,128]{2,1,0:T(8,128)S(1)}, u32[]{:S(2)}, u32[]{:S(2)}) collective-permute-start(f32[48,8,128]{2,1,0:T(8,128)S(1)} %get-tuple-element.31), channel_id=1, source_target_pairs={{0,16},{1,17},{2,18},{3,19},{4,20},{5,21},{6,22},{7,23},{8,24},{9,... | collective-permute-start | bytes 589832 | tf_op jit(solution)/shard_map/ppermute | solution.py:64
  4.8 1.8 %collective-permute-start.4 = (f32[12,8,128]{2,1,0:T(8,128)S(1)}, f32[12,8,128]{2,1,0:T(8,128)S(1)}, u32[]{:S(2)}, u32[]{:S(2)}) collective-permute-start(f32[12,8,128]{2,1,0:T(8,128)S(1)} %get-tuple-element.35), channel_id=1, source_target_pairs={{0,1},{1,0},{2,3},{3,2},{4,5},{5,4},{6,7},{7,6},{8,9},{9,8},{10,11... | collective-permute-start | bytes 147464 | tf_op jit(solution)/shard_map/ppermute | solution.py:64
  4.8 13.7 %collective-permute-start.2 = (f32[64,8,128]{2,1,0:T(8,128)S(1)}, f32[64,8,128]{2,1,0:T(8,128)S(1)}, u32[]{:S(2)}, u32[]{:S(2)}) collective-permute-start(f32[64,8,128]{2,1,0:T(8,128)S(1)} %get-tuple-element.33), channel_id=1, source_target_pairs={{0,4},{1,5},{2,6},{3,7},{4,0},{5,1},{6,2},{7,3},{8,12},{9,13},{10,... | collective-permute-start | bytes 786440 | tf_op jit(solution)/shard_map/ppermute | solution.py:64
  6.4 12.2 %collective-permute-start.3 = (f32[64,8,128]{2,1,0:T(8,128)S(1)}, f32[64,8,128]{2,1,0:T(8,128)S(1)}, u32[]{:S(2)}, u32[]{:S(2)}) collective-permute-start(f32[64,8,128]{2,1,0:T(8,128)S(1)} %get-tuple-element.34), channel_id=1, source_target_pairs={{0,1},{1,0},{2,3},{3,2},{4,8},{5,9},{6,10},{7,11},{8,4},{9,5},{10,... | collective-permute-start | bytes 786440 | tf_op jit(solution)/shard_map/ppermute | solution.py:64
  6.6 4.2 %collective-permute-start.5 = (f32[12,8,128]{2,1,0:T(8,128)S(1)}, f32[12,8,128]{2,1,0:T(8,128)S(1)}, u32[]{:S(2)}, u32[]{:S(2)}) collective-permute-start(f32[12,8,128]{2,1,0:T(8,128)S(1)} %add.6.refs_0_), channel_id=1, source_target_pairs={{0,2},{1,3},{2,0},{3,1},{4,6},{5,7},{6,4},{7,5},{8,10},{9,11},{10,... | collective-permute-start | bytes 147464 | tf_op jit(solution)/shard_map/ppermute | solution.py:64
  8.2 0.8 %copy-start.1 = (f32[8,12,128]{2,0,1:T(8,128)S(1)}, f32[8,12,128]{2,0,1:T(8,128)}, u32[]{:S(2)}) copy-start(f32[8,12,128]{2,0,1:T(8,128)} %param.3) | copy-start | bytes 147460
  10.8 4.7 %collective-permute-start.6 = (f32[12,8,128]{2,1,0:T(8,128)S(1)}, f32[12,8,128]{2,1,0:T(8,128)S(1)}, u32[]{:S(2)}, u32[]{:S(2)}) collective-permute-start(f32[12,8,128]{2,1,0:T(8,128)S(1)} %shard_map.43.refs_5_.v_here), channel_id=1, source_target_pairs={{0,16},{1,17},{2,18},{3,19},{4,20},{5,21},{6,22},{7,23},{8,24},{9,... | collective-permute-start | bytes 147464 | tf_op jit(solution)/shard_map/ppermute | solution.py:64
  11.4 7.1 %collective-permute-start.1 = (f32[48,8,128]{2,1,0:T(8,128)S(1)}, f32[48,8,128]{2,1,0:T(8,128)S(1)}, u32[]{:S(2)}, u32[]{:S(2)}) collective-permute-start(f32[48,8,128]{2,1,0:T(8,128)S(1)} %get-tuple-element.32), channel_id=1, source_target_pairs={{0,16},{1,17},{2,18},{3,19},{4,20},{5,21},{6,22},{7,23},{8,24},{9,... | collective-permute-start | bytes 589832 | tf_op jit(solution)/shard_map/ppermute | solution.py:64
  15.5 6.1 %collective-permute-start.7 = (f32[36,8,128]{2,1,0:T(8,128)S(1)}, f32[36,8,128]{2,1,0:T(8,128)S(1)}, u32[]{:S(2)}, u32[]{:S(2)}) collective-permute-start(f32[36,8,128]{2,1,0:T(8,128)S(1)} %get-tuple-element.41), channel_id=1, source_target_pairs={{0,4},{1,5},{2,6},{3,7},{4,0},{5,1},{6,2},{7,3},{8,12},{9,13},{10,... | collective-permute-start | bytes 442376 | tf_op jit(solution)/shard_map/ppermute | solution.py:64
  18.5 3.1 %collective-permute-start.8 = (f32[36,8,128]{2,1,0:T(8,128)S(1)}, f32[36,8,128]{2,1,0:T(8,128)S(1)}, u32[]{:S(2)}, u32[]{:S(2)}) collective-permute-start(f32[36,8,128]{2,1,0:T(8,128)S(1)} %get-tuple-element.42), channel_id=1, source_target_pairs={{0,1},{1,0},{2,3},{3,2},{4,8},{5,9},{6,10},{7,11},{8,4},{9,5},{10,... | collective-permute-start | bytes 442376 | tf_op jit(solution)/shard_map/ppermute | solution.py:64
  23.9 12.4 %collective-permute-start.9 = (f32[48,8,128]{2,1,0:T(8,128)S(1)}, f32[48,8,128]{2,1,0:T(8,128)S(1)}, u32[]{:S(2)}, u32[]{:S(2)}) collective-permute-start(f32[48,8,128]{2,1,0:T(8,128)S(1)} %get-tuple-element.44), channel_id=1, source_target_pairs={{0,16},{1,17},{2,18},{3,19},{4,20},{5,21},{6,22},{7,23},{8,24},{9,... | collective-permute-start | bytes 589832 | tf_op jit(solution)/shard_map/ppermute | solution.py:64
  24.6 2.3 %collective-permute-start.13 = (f32[12,8,128]{2,1,0:T(8,128)S(1)}, f32[12,8,128]{2,1,0:T(8,128)S(1)}, u32[]{:S(2)}, u32[]{:S(2)}) collective-permute-start(f32[12,8,128]{2,1,0:T(8,128)S(1)} %get-tuple-element.48), channel_id=1, source_target_pairs={{0,1},{1,0},{2,3},{3,2},{4,5},{5,4},{6,7},{7,6},{8,9},{9,8},{10,11... | collective-permute-start | bytes 147464 | tf_op jit(solution)/shard_map/ppermute | solution.py:64
  24.6 12.7 %collective-permute-start.11 = (f32[64,8,128]{2,1,0:T(8,128)S(1)}, f32[64,8,128]{2,1,0:T(8,128)S(1)}, u32[]{:S(2)}, u32[]{:S(2)}) collective-permute-start(f32[64,8,128]{2,1,0:T(8,128)S(1)} %get-tuple-element.46), channel_id=1, source_target_pairs={{0,4},{1,5},{2,6},{3,7},{4,0},{5,1},{6,2},{7,3},{8,12},{9,13},{10,... | collective-permute-start | bytes 786440 | tf_op jit(solution)/shard_map/ppermute | solution.py:64
  26.6 10.7 %collective-permute-start.12 = (f32[64,8,128]{2,1,0:T(8,128)S(1)}, f32[64,8,128]{2,1,0:T(8,128)S(1)}, u32[]{:S(2)}, u32[]{:S(2)}) collective-permute-start(f32[64,8,128]{2,1,0:T(8,128)S(1)} %get-tuple-element.47), channel_id=1, source_target_pairs={{0,1},{1,0},{2,3},{3,2},{4,8},{5,9},{6,10},{7,11},{8,4},{9,5},{10,... | collective-permute-start | bytes 786440 | tf_op jit(solution)/shard_map/ppermute | solution.py:64
  26.9 4.2 %collective-permute-start.14 = (f32[12,8,128]{2,1,0:T(8,128)S(1)}, f32[12,8,128]{2,1,0:T(8,128)S(1)}, u32[]{:S(2)}, u32[]{:S(2)}) collective-permute-start(f32[12,8,128]{2,1,0:T(8,128)S(1)} %add.7.refs_0_), channel_id=1, source_target_pairs={{0,2},{1,3},{2,0},{3,1},{4,6},{5,7},{6,4},{7,5},{8,10},{9,11},{10,... | collective-permute-start | bytes 147464 | tf_op jit(solution)/shard_map/ppermute | solution.py:64
  28.4 8.8 %collective-permute-start.10 = (f32[48,8,128]{2,1,0:T(8,128)S(1)}, f32[48,8,128]{2,1,0:T(8,128)S(1)}, u32[]{:S(2)}, u32[]{:S(2)}) collective-permute-start(f32[48,8,128]{2,1,0:T(8,128)S(1)} %get-tuple-element.45), channel_id=1, source_target_pairs={{0,16},{1,17},{2,18},{3,19},{4,20},{5,21},{6,22},{7,23},{8,24},{9,... | collective-permute-start | bytes 589832 | tf_op jit(solution)/shard_map/ppermute | solution.py:64
  31.1 5.2 %collective-permute-start.15 = (f32[12,8,128]{2,1,0:T(8,128)S(1)}, f32[12,8,128]{2,1,0:T(8,128)S(1)}, u32[]{:S(2)}, u32[]{:S(2)}) collective-permute-start(f32[12,8,128]{2,1,0:T(8,128)S(1)} %shard_map.47.refs_5_.v_here.refs_7_), channel_id=1, source_target_pairs={{0,16},{1,17},{2,18},{3,19},{4,20},{5,21},{6,22},{7,23},{8,24},{9,... | collective-permute-start | bytes 147464 | tf_op jit(solution)/shard_map/ppermute | solution.py:64
  36.3 5.2 %collective-permute-start.16 = (f32[36,8,128]{2,1,0:T(8,128)S(1)}, f32[36,8,128]{2,1,0:T(8,128)S(1)}, u32[]{:S(2)}, u32[]{:S(2)}) collective-permute-start(f32[36,8,128]{2,1,0:T(8,128)S(1)} %get-tuple-element.54), channel_id=1, source_target_pairs={{0,4},{1,5},{2,6},{3,7},{4,0},{5,1},{6,2},{7,3},{8,12},{9,13},{10,... | collective-permute-start | bytes 442376 | tf_op jit(solution)/shard_map/ppermute | solution.py:64
  37.3 4.3 %collective-permute-start.17 = (f32[36,8,128]{2,1,0:T(8,128)S(1)}, f32[36,8,128]{2,1,0:T(8,128)S(1)}, u32[]{:S(2)}, u32[]{:S(2)}) collective-permute-start(f32[36,8,128]{2,1,0:T(8,128)S(1)} %get-tuple-element.55), channel_id=1, source_target_pairs={{0,1},{1,0},{2,3},{3,2},{4,8},{5,9},{6,10},{7,11},{8,4},{9,5},{10,... | collective-permute-start | bytes 442376 | tf_op jit(solution)/shard_map/ppermute | solution.py:64

commit v4 on v3

--- a/solution.py
+++ b/solution.py
@@ -41,7 +41,7 @@
         self.ext_cols = self.cols + 2 * WIDE
         self.corner = sum(corner_depth(d) for d in range(1, WIDE - 1))
         self.v_cols = WIDE // 2
-        self.edge_cells = len(self.xs) * (self.corner + self.v_cols) + WIDE
+        self.edge_cells = len(self.xs) * (self.corner + self.v_cols) + WIDE - 2
         depth = [min(c + 1, self.cols - c) for c in range(self.cols)]
         self.soon = [corner_depth(d) if d < WIDE - 1 else 0 for d in depth]
         self.soon_at = [sum(self.soon[:c]) for c in range(self.cols + 1)]
@@ -135,9 +135,9 @@
     v_there, soon, out = refs[:nx], refs[nx : 2 * nx], refs[2 * nx :]
     for ky, o in zip(plan.ys, out):
         hi = plan.above("gy", ky)
-        o[0:WIDE] = v_here[pl.ds(plan.near(hi, WIDE, plan.cols), WIDE)]
+        o[0 : WIDE - 2] = v_here[pl.ds(plan.near(hi, WIDE - 2, plan.cols), WIDE - 2)]
         for n in range(nx):
-            at = WIDE + n * (plan.v_cols + plan.corner)
+            at = WIDE - 2 + n * (plan.v_cols + plan.corner)
             o[at : at + plan.v_cols] = v_there[n][pl.ds(plan.near(hi, plan.v_cols, plan.cols), plan.v_cols)]
             at += plan.v_cols
             base = jnp.where(hi, plan.soon_at[-1] - plan.corner, 0)
@@ -151,14 +151,14 @@
         apart = lax.broadcasted_iota(jnp.int32, (LANES, LANES), 0) - lax.broadcasted_iota(jnp.int32, (LANES, LANES), 1)
         apart = jnp.abs(apart)
         weights = jnp.where(apart == 1, -16.0, jnp.where(apart == 2, 1.0, 0.0))
-        self.weights = weights.astype(jnp.bfloat16)
+        self.weights = jnp.concatenate([weights, weights], axis=0).astype(jnp.bfloat16)
 
     def along_z(self, cells):
         flat = cells.reshape(-1, LANES)
         high = flat.astype(jnp.bfloat16)
         low = (flat - high.astype(jnp.float32)).astype(jnp.bfloat16)
-        times = lambda v: jnp.dot(v, self.weights, preferred_element_type=jnp.float32)
-        return (times(high) + times(low)).reshape(cells.shape)
+        both = jnp.concatenate([high, low], axis=1)
+        return jnp.dot(both, self.weights, preferred_element_type=jnp.float32).reshape(cells.shape)
 
     def put_potential(self, first, v, count):
         scaled = 24.0 * v + 90.0
@@ -281,16 +281,17 @@
     else:
         half_ref, dens_ref = take(2)
         packed = take(ny + 2 * nx)
+        (flat,) = take(1)
     rows, cols, f, long = plan.rows, plan.cols, plan.fields, plan.ext_rows
     steps = Steps(plan, levels, pot)
     h0 = levels[0]
     for n, ky in enumerate(plan.ys):
         hi = plan.above("gy", ky)
-        base = plan.beyond(hi, WIDE, cols)
-        for c in range(WIDE):
+        base = plan.beyond(hi, WIDE - 2, cols)
+        for c in range(WIDE - 2):
             steps.put_potential((base + c) * long + WIDE, edge[n][c], rows)
         for n_x, kx in enumerate(plan.xs):
-            at = WIDE + n_x * (plan.v_cols + plan.corner)
+            at = WIDE - 2 + n_x * (plan.v_cols + plan.corner)
             x_hi = plan.above("gx", kx)
             row, src = plan.beyond(x_hi, WIDE, rows), plan.at_partner(x_hi, WIDE, rows)
             first = plan.beyond(hi, plan.v_cols, cols)
@@ -329,10 +330,10 @@
     def total(s, g):
         a = [(s / 24.0) ** k for k in range(ORDER + 1)]
         even = g[0] - (a[2] / 2) * g[2] + (a[4] / 24) * g[4]
-        odd = a[1] * g[1] - (a[3] / 6) * g[3]
-        return even + sign * pltpu.roll(odd, plan.bands, 0)
-
-    @pl.loop(0, cols, unroll=divisor(cols, 6))
+        odd = (a[3] / 6 * sign) * g[3] - (a[1] * sign) * g[1]
+        return even + pltpu.roll(odd, plan.bands, 0)
+
+    @pl.loop(0, cols, unroll=divisor(cols, 12))
     def _(c):
         def finish(at, t, value):
             g = [h[at] for h in levels] + [value]
@@ -343,7 +344,7 @@
             else:
                 half_ref[cell] = half
                 full = total(step_length, g)
-                dens_ref[c, t : t + 1, :] = jnp.sum(full * full, axis=0, keepdims=True)
+                flat[pl.ds(pl.multiple_of(cell * f, f), f), :] = full * full
 
         steps.image(levels[-1], (WIDE + c) * long + WIDE, rows, finish)
 
@@ -355,6 +356,11 @@
                     first = c * rows * f + p * plan.bands + b
                     orb_ref[p, b, c] = flat[pl.ds(first, rows, stride=f), :]
     else:
+        for c in range(cols):
+            parts = [flat[pl.ds(c * rows * f + n, rows, stride=f), :] for n in range(f)]
+            while len(parts) > 1:
+                parts = [sum(parts[n : n + 2]) for n in range(0, len(parts), 2)]
+            dens_ref[c] = parts[0]
         pack(plan, half_ref, packed)
 
 
@@ -405,7 +411,7 @@
             dens = dens + swap(dens, flip=1)
             more = [swap(dens, flip=b) for b in range(2, plan.groups, 2)]
             (v_here,) = call(potential_kernel, [plane])(external, dens, *more)
-            v_there = [swap(v_here, kx=k) for k in plan.xs]
+            v_there = [swap(v_here, kx=k, flip=1) for k in plan.xs]
             edge = call(
                 functools.partial(edge_kernel, plan), [(plan.edge_cells, f, LANES)] * ny
             )(v_here, *v_there, *soon)
@@ -420,6 +426,7 @@
         half, dens, *out = call(
             functools.partial(evolve_kernel, plan, False),
             blocks + [field_shape, plane] + packed,
+            [pltpu.VMEM((cells * f, LANES), jnp.float32)],
             limit=4,
             alias=len(blocks),
         )(*arrived)[len(blocks) :]

time: 44.6 us -> 44.7 us (level)
  waiting for transfers between devices: 14 us -> 17.6 us
  starting transfers between devices: 19.9 us -> 17.5 us
  Pallas kernels: 7.95 us -> 6.83 us
    ppermute x18, waiting for transfers between devices: 14 us -> 17.6 us  [swap(): return lax.ppermute(value, AXES, self.pairs(**kinds))]
    ppermute x18, starting transfers between devices: 19.9 us -> 17.5 us  [swap(): return lax.ppermute(value, AXES, self.pairs(**kinds))]
    pallas_call x10, Pallas kernels: 7.95 us -> 6.83 us  [call(): pl.pallas_call(kernel, out_shape=[jax.ShapeDtypeStruct(s, jnp.float32) fo...]
  transfers between devices with their start and end apart: 18 -> 18, of which waited for: 6 -> 6; matrix products, arithmetic and copies ran while one was open for 0% -> 0% of each run, Pallas kernels for 6% -> 5%
where the time goes in v4:
time: 44.7 us; the launch traced here: 44.4 us
  waiting for transfers between devices  17.6 us (39%)
  starting transfers between devices  17.5 us (39%)
  Pallas kernels  6.83 us (15%)
  local copies, waits for them, and re-layouts  1.79 us (4%)
  between operations  0.71 us (2%)
    ppermute x18, waiting for transfers between devices, swap(): return lax.ppermute(value, AXES, self.pairs(**kinds))  17.6 us
    ppermute x18, starting transfers between devices, swap(): return lax.ppermute(value, AXES, self.pairs(**kinds))  17.5 us
    pallas_call x10, Pallas kernels, call(): pl.pallas_call(kernel, out_shape=[jax.ShapeDtypeStruct(s, jnp.float32) fo...  6.83 us
    unnamed x4, local copies, waits for them, and re-layouts  1.79 us
  transfers between devices with their start and end apart: 18, of which 6 were waited for; matrix products, arithmetic and copies ran while one was open for 0% of the time, Pallas kernels for 5%

profile of v4, /device:TPU:0, one launch (start us, length us, event | category | flops | bytes accessed | tf_op | source)
XLA Modules:
  0.0 44.4 jit_solution(10318409782304848199)
XLA Ops:
  0.6 1.0 %copy-done = f32[2,4,8,12,128]{4,2,3,1,0:T(8,128)S(1)} copy-done((f32[2,4,8,12,128]{4,2,3,1,0:T(8,128)S(1)}, f32[2,4,8,12,128]{4,2,3,1,0:T(8,128)}, u32[]{:S(2)}) %copy-start) | copy-done | bytes 393240
  1.8 3.0 %collective-permute-start = (f32[48,8,128]{2,1,0:T(8,128)S(1)}, f32[48,8,128]{2,1,0:T(8,128)S(1)}, u32[]{:S(2)}, u32[]{:S(2)}) collective-permute-start(f32[48,8,128]{2,1,0:T(8,128)S(1)} %get-tuple-element.31), channel_id=1, source_target_pairs={{0,16},{1,17},{2,18},{3,19},{4,20},{5,21},{6,22},{7,23},{8,24},{9,... | collective-permute-start | bytes 589832 | tf_op jit(solution)/shard_map/ppermute | solution.py:64
  4.8 1.6 %collective-permute-start.2 = (f32[64,8,128]{2,1,0:T(8,128)S(1)}, f32[64,8,128]{2,1,0:T(8,128)S(1)}, u32[]{:S(2)}, u32[]{:S(2)}) collective-permute-start(f32[64,8,128]{2,1,0:T(8,128)S(1)} %get-tuple-element.33), channel_id=1, source_target_pairs={{0,4},{1,5},{2,6},{3,7},{4,0},{5,1},{6,2},{7,3},{8,12},{9,13},{10,... | collective-permute-start | bytes 786440 | tf_op jit(solution)/shard_map/ppermute | solution.py:64
  6.6 1.6 %collective-permute-start.5 = (f32[12,8,128]{2,1,0:T(8,128)S(1)}, f32[12,8,128]{2,1,0:T(8,128)S(1)}, u32[]{:S(2)}, u32[]{:S(2)}) collective-permute-start(f32[12,8,128]{2,1,0:T(8,128)S(1)} %add.6.refs_0_), channel_id=1, source_target_pairs={{0,2},{1,3},{2,0},{3,1},{4,6},{5,7},{6,4},{7,5},{8,10},{9,11},{10,... | collective-permute-start | bytes 147464 | tf_op jit(solution)/shard_map/ppermute | solution.py:64
  8.2 0.5 %collective-permute-start.1 = (f32[48,8,128]{2,1,0:T(8,128)S(1)}, f32[48,8,128]{2,1,0:T(8,128)S(1)}, u32[]{:S(2)}, u32[]{:S(2)}) collective-permute-start(f32[48,8,128]{2,1,0:T(8,128)S(1)} %get-tuple-element.32), channel_id=1, source_target_pairs={{0,16},{1,17},{2,18},{3,19},{4,20},{5,21},{6,22},{7,23},{8,24},{9,... | collective-permute-start | bytes 589832 | tf_op jit(solution)/shard_map/ppermute | solution.py:64
  8.8 0.8 %copy-done.1 = f32[8,12,128]{2,0,1:T(8,128)S(1)} copy-done((f32[8,12,128]{2,0,1:T(8,128)S(1)}, f32[8,12,128]{2,0,1:T(8,128)}, u32[]{:S(2)}) %copy-start.1) | copy-done | bytes 49176
  9.6 1.2 %collective-permute-done.5.refs_1_ = f32[12,8,128]{2,1,0:T(8,128)S(1)} collective-permute-done((f32[12,8,128]{2,1,0:T(8,128)S(1)}, f32[12,8,128]{2,1,0:T(8,128)S(1)}, u32[]{:S(2)}, u32[]{:S(2)}) %collective-permute-start.5) | collective-permute-done | bytes 49184 | tf_op jit(solution)/shard_map/ppermute | solution.py:64
  10.9 4.2 %collective-permute-done.6.refs_6_.refs_0_ = f32[12,8,128]{2,1,0:T(8,128)S(1)} collective-permute-done((f32[12,8,128]{2,1,0:T(8,128)S(1)}, f32[12,8,128]{2,1,0:T(8,128)S(1)}, u32[]{:S(2)}, u32[]{:S(2)}) %collective-permute-start.6) | collective-permute-done | bytes 49184 | tf_op jit(solution)/shard_map/ppermute | solution.py:64
  15.1 2.8 %collective-permute-start.7 = (f32[34,8,128]{2,1,0:T(8,128)S(1)}, f32[34,8,128]{2,1,0:T(8,128)S(1)}, u32[]{:S(2)}, u32[]{:S(2)}) collective-permute-start(f32[34,8,128]{2,1,0:T(8,128)S(1)} %get-tuple-element.41), channel_id=1, source_target_pairs={{0,4},{1,5},{2,6},{3,7},{4,0},{5,1},{6,2},{7,3},{8,12},{9,13},{10,... | collective-permute-start | bytes 417800 | tf_op jit(solution)/shard_map/ppermute | solution.py:64
  18.0 0.3 collective-permute-start.8
  18.3 1.1 %shard_map.44 = (f32[672,8,128]{2,1,0:T(8,128)S(1)}, f32[672,8,128]{2,1,0:T(8,128)S(1)}, f32[672,8,128]{2,1,0:T(8,128)S(1)}, f32[672,8,128]{2,1,0:T(8,128)S(1)}, f32[672,8,128]{2,1,0:T(8,128)S(1)}) custom-call(f32[96,8,128]{2,1,0:T(8,128)S(1)} %get-tuple-element.30.refs_0_, f32[48,8,128]{2,1,0:T(8,128)S(1)} %collective-permute-done.refs_1_, ...), custom_call_target="tpu_custom_call" | custom-call | tf_op jit(solution)/shard_map/pallas_call | solution.py:369
  19.5 3.0 %collective-permute-done.7.refs_5_ = f32[34,8,128]{2,1,0:T(8,128)S(1)} collective-permute-done((f32[34,8,128]{2,1,0:T(8,128)S(1)}, f32[34,8,128]{2,1,0:T(8,128)S(1)}, u32[]{:S(2)}, u32[]{:S(2)}) %collective-permute-start.7) | collective-permute-done | bytes 139296 | tf_op jit(solution)/shard_map/ppermute | solution.py:64
  22.4 1.9 %shard_map.46 = (f32[672,8,128]{2,1,0:T(8,128)S(1)}, f32[672,8,128]{2,1,0:T(8,128)S(1)}, f32[672,8,128]{2,1,0:T(8,128)S(1)}, f32[672,8,128]{2,1,0:T(8,128)S(1)},...) custom-call(f32[672,8,128]{2,1,0:T(8,128)S(1)} %get-tuple-element.36, ...), custom_call_target="tpu_custom_call", output_to_operand_aliasing={{0}: (0, {}), {1}: (1, {}), {2}: (2, {}), {3}: (3, {}), {4}... | custom-call | tf_op jit(solution)/shard_map/pallas_call | solution.py:369
  24.3 0.6 %collective-permute-start.9 = (f32[48,8,128]{2,1,0:T(8,128)S(1)}, f32[48,8,128]{2,1,0:T(8,128)S(1)}, u32[]{:S(2)}, u32[]{:S(2)}) collective-permute-start(f32[48,8,128]{2,1,0:T(8,128)S(1)} %get-tuple-element.44), channel_id=1, source_target_pairs={{0,16},{1,17},{2,18},{3,19},{4,20},{5,21},{6,22},{7,23},{8,24},{9,... | collective-permute-start | bytes 589832 | tf_op jit(solution)/shard_map/ppermute | solution.py:64
  25.0 1.9 %collective-permute-start.11 = (f32[64,8,128]{2,1,0:T(8,128)S(1)}, f32[64,8,128]{2,1,0:T(8,128)S(1)}, u32[]{:S(2)}, u32[]{:S(2)}) collective-permute-start(f32[64,8,128]{2,1,0:T(8,128)S(1)} %get-tuple-element.46), channel_id=1, source_target_pairs={{0,4},{1,5},{2,6},{3,7},{4,0},{5,1},{6,2},{7,3},{8,12},{9,13},{10,... | collective-permute-start | bytes 786440 | tf_op jit(solution)/shard_map/ppermute | solution.py:64
  27.1 1.6 %collective-permute-start.14 = (f32[12,8,128]{2,1,0:T(8,128)S(1)}, f32[12,8,128]{2,1,0:T(8,128)S(1)}, u32[]{:S(2)}, u32[]{:S(2)}) collective-permute-start(f32[12,8,128]{2,1,0:T(8,128)S(1)} %add.7.refs_0_), channel_id=1, source_target_pairs={{0,2},{1,3},{2,0},{3,1},{4,6},{5,7},{6,4},{7,5},{8,10},{9,11},{10,... | collective-permute-start | bytes 147464 | tf_op jit(solution)/shard_map/ppermute | solution.py:64
  28.7 0.5 %collective-permute-start.10 = (f32[48,8,128]{2,1,0:T(8,128)S(1)}, f32[48,8,128]{2,1,0:T(8,128)S(1)}, u32[]{:S(2)}, u32[]{:S(2)}) collective-permute-start(f32[48,8,128]{2,1,0:T(8,128)S(1)} %get-tuple-element.45), channel_id=1, source_target_pairs={{0,16},{1,17},{2,18},{3,19},{4,20},{5,21},{6,22},{7,23},{8,24},{9,... | collective-permute-start | bytes 589832 | tf_op jit(solution)/shard_map/ppermute | solution.py:64
  29.2 2.1 %collective-permute-done.14.refs_1_ = f32[12,8,128]{2,1,0:T(8,128)S(1)} collective-permute-done((f32[12,8,128]{2,1,0:T(8,128)S(1)}, f32[12,8,128]{2,1,0:T(8,128)S(1)}, u32[]{:S(2)}, u32[]{:S(2)}) %collective-permute-start.14) | collective-permute-done | bytes 49184 | tf_op jit(solution)/shard_map/ppermute | solution.py:64
  31.3 0.4 collective-permute-start.15
  31.7 3.9 %collective-permute-done.15.refs_6_.refs_0_ = f32[12,8,128]{2,1,0:T(8,128)S(1)} collective-permute-done((f32[12,8,128]{2,1,0:T(8,128)S(1)}, f32[12,8,128]{2,1,0:T(8,128)S(1)}, u32[]{:S(2)}, u32[]{:S(2)}) %collective-permute-start.15) | collective-permute-done | bytes 49184 | tf_op jit(solution)/shard_map/ppermute | solution.py:64
  35.6 1.7 %collective-permute-start.16 = (f32[34,8,128]{2,1,0:T(8,128)S(1)}, f32[34,8,128]{2,1,0:T(8,128)S(1)}, u32[]{:S(2)}, u32[]{:S(2)}) collective-permute-start(f32[34,8,128]{2,1,0:T(8,128)S(1)} %get-tuple-element.54), channel_id=1, source_target_pairs={{0,4},{1,5},{2,6},{3,7},{4,0},{5,1},{6,2},{7,3},{8,12},{9,13},{10,... | collective-permute-start | bytes 417800 | tf_op jit(solution)/shard_map/ppermute | solution.py:64
  37.7 1.1 %shard_map.48 = (f32[672,8,128]{2,1,0:T(8,128)S(1)}, f32[672,8,128]{2,1,0:T(8,128)S(1)}, f32[672,8,128]{2,1,0:T(8,128)S(1)}, f32[672,8,128]{2,1,0:T(8,128)S(1)}, f32[672,8,128]{2,1,0:T(8,128)S(1)}) custom-call(f32[96,8,128]{2,1,0:T(8,128)S(1)} %get-tuple-element.43.refs_0_, f32[48,8,128]{2,1,0:T(8,128)S(1)} %collective-permute-done.9.refs_1_, ...), custom_call_target="tpu_custom_call" | custom-call | tf_op jit(solution)/shard_map/pallas_call | solution.py:369
  38.9 3.2 %collective-permute-done.16.refs_5_ = f32[34,8,128]{2,1,0:T(8,128)S(1)} collective-permute-done((f32[34,8,128]{2,1,0:T(8,128)S(1)}, f32[34,8,128]{2,1,0:T(8,128)S(1)}, u32[]{:S(2)}, u32[]{:S(2)}) %collective-permute-start.16) | collective-permute-done | bytes 139296 | tf_op jit(solution)/shard_map/ppermute | solution.py:64
  42.1 2.4 %shard_map.50 = (f32[672,8,128]{2,1,0:T(8,128)S(1)}, f32[672,8,128]{2,1,0:T(8,128)S(1)}, f32[672,8,128]{2,1,0:T(8,128)S(1)}, f32[672,8,128]{2,1,0:T(8,128)S(1)},...) custom-call(f32[672,8,128]{2,1,0:T(8,128)S(1)} %get-tuple-element.49, ...), custom_call_target="tpu_custom_call", output_to_operand_aliasing={{0}: (0, {}), {1}: (1, {}), {2}: (2, {}), {3}: (3, {}), {4}... | custom-call | tf_op jit(solution)/shard_map/pallas_call | solution.py:369
  (28 shorter events, 1.2 us)
Async XLA Ops:
  0.6 1.0 %copy-start = (f32[2,4,8,12,128]{4,2,3,1,0:T(8,128)S(1)}, f32[2,4,8,12,128]{4,2,3,1,0:T(8,128)}, u32[]{:S(2)}) copy-start(f32[2,4,8,12,128]{4,2,3,1,0:T(8,128)} %param.2) | copy-start | bytes 1179652
  1.8 13.3 %collective-permute-start = (f32[48,8,128]{2,1,0:T(8,128)S(1)}, f32[48,8,128]{2,1,0:T(8,128)S(1)}, u32[]{:S(2)}, u32[]{:S(2)}) collective-permute-start(f32[48,8,128]{2,1,0:T(8,128)S(1)} %get-tuple-element.31), channel_id=1, source_target_pairs={{0,16},{1,17},{2,18},{3,19},{4,20},{5,21},{6,22},{7,23},{8,24},{9,... | collective-permute-start | bytes 589832 | tf_op jit(solution)/shard_map/ppermute | solution.py:64
  4.8 1.8 %collective-permute-start.4 = (f32[12,8,128]{2,1,0:T(8,128)S(1)}, f32[12,8,128]{2,1,0:T(8,128)S(1)}, u32[]{:S(2)}, u32[]{:S(2)}) collective-permute-start(f32[12,8,128]{2,1,0:T(8,128)S(1)} %get-tuple-element.35), channel_id=1, source_target_pairs={{0,1},{1,0},{2,3},{3,2},{4,5},{5,4},{6,7},{7,6},{8,9},{9,8},{10,11... | collective-permute-start | bytes 147464 | tf_op jit(solution)/shard_map/ppermute | solution.py:64
  4.8 13.5 %collective-permute-start.2 = (f32[64,8,128]{2,1,0:T(8,128)S(1)}, f32[64,8,128]{2,1,0:T(8,128)S(1)}, u32[]{:S(2)}, u32[]{:S(2)}) collective-permute-start(f32[64,8,128]{2,1,0:T(8,128)S(1)} %get-tuple-element.33), channel_id=1, source_target_pairs={{0,4},{1,5},{2,6},{3,7},{4,0},{5,1},{6,2},{7,3},{8,12},{9,13},{10,... | collective-permute-start | bytes 786440 | tf_op jit(solution)/shard_map/ppermute | solution.py:64
  6.4 11.9 %collective-permute-start.3 = (f32[64,8,128]{2,1,0:T(8,128)S(1)}, f32[64,8,128]{2,1,0:T(8,128)S(1)}, u32[]{:S(2)}, u32[]{:S(2)}) collective-permute-start(f32[64,8,128]{2,1,0:T(8,128)S(1)} %get-tuple-element.34), channel_id=1, source_target_pairs={{0,1},{1,0},{2,3},{3,2},{4,8},{5,9},{6,10},{7,11},{8,4},{9,5},{10,... | collective-permute-start | bytes 786440 | tf_op jit(solution)/shard_map/ppermute | solution.py:64
  6.6 4.2 %collective-permute-start.5 = (f32[12,8,128]{2,1,0:T(8,128)S(1)}, f32[12,8,128]{2,1,0:T(8,128)S(1)}, u32[]{:S(2)}, u32[]{:S(2)}) collective-permute-start(f32[12,8,128]{2,1,0:T(8,128)S(1)} %add.6.refs_0_), channel_id=1, source_target_pairs={{0,2},{1,3},{2,0},{3,1},{4,6},{5,7},{6,4},{7,5},{8,10},{9,11},{10,... | collective-permute-start | bytes 147464 | tf_op jit(solution)/shard_map/ppermute | solution.py:64
  8.2 10.1 %collective-permute-start.1 = (f32[48,8,128]{2,1,0:T(8,128)S(1)}, f32[48,8,128]{2,1,0:T(8,128)S(1)}, u32[]{:S(2)}, u32[]{:S(2)}) collective-permute-start(f32[48,8,128]{2,1,0:T(8,128)S(1)} %get-tuple-element.32), channel_id=1, source_target_pairs={{0,16},{1,17},{2,18},{3,19},{4,20},{5,21},{6,22},{7,23},{8,24},{9,... | collective-permute-start | bytes 589832 | tf_op jit(solution)/shard_map/ppermute | solution.py:64
  8.8 0.8 %copy-start.1 = (f32[8,12,128]{2,0,1:T(8,128)S(1)}, f32[8,12,128]{2,0,1:T(8,128)}, u32[]{:S(2)}) copy-start(f32[8,12,128]{2,0,1:T(8,128)} %param.3) | copy-start | bytes 147460
  10.8 4.3 %collective-permute-start.6 = (f32[12,8,128]{2,1,0:T(8,128)S(1)}, f32[12,8,128]{2,1,0:T(8,128)S(1)}, u32[]{:S(2)}, u32[]{:S(2)}) collective-permute-start(f32[12,8,128]{2,1,0:T(8,128)S(1)} %shard_map.43.refs_5_.v_here), channel_id=1, source_target_pairs={{0,17},{1,16},{2,19},{3,18},{4,21},{5,20},{6,23},{7,22},{8,25},{9,... | collective-permute-start | bytes 147464 | tf_op jit(solution)/shard_map/ppermute | solution.py:64
  15.1 7.3 %collective-permute-start.7 = (f32[34,8,128]{2,1,0:T(8,128)S(1)}, f32[34,8,128]{2,1,0:T(8,128)S(1)}, u32[]{:S(2)}, u32[]{:S(2)}) collective-permute-start(f32[34,8,128]{2,1,0:T(8,128)S(1)} %get-tuple-element.41), channel_id=1, source_target_pairs={{0,4},{1,5},{2,6},{3,7},{4,0},{5,1},{6,2},{7,3},{8,12},{9,13},{10,... | collective-permute-start | bytes 417800 | tf_op jit(solution)/shard_map/ppermute | solution.py:64
  18.0 4.5 %collective-permute-start.8 = (f32[34,8,128]{2,1,0:T(8,128)S(1)}, f32[34,8,128]{2,1,0:T(8,128)S(1)}, u32[]{:S(2)}, u32[]{:S(2)}) collective-permute-start(f32[34,8,128]{2,1,0:T(8,128)S(1)} %get-tuple-element.42), channel_id=1, source_target_pairs={{0,1},{1,0},{2,3},{3,2},{4,8},{5,9},{6,10},{7,11},{8,4},{9,5},{10,... | collective-permute-start | bytes 417800 | tf_op jit(solution)/shard_map/ppermute | solution.py:64
  24.3 11.3 %collective-permute-start.9 = (f32[48,8,128]{2,1,0:T(8,128)S(1)}, f32[48,8,128]{2,1,0:T(8,128)S(1)}, u32[]{:S(2)}, u32[]{:S(2)}) collective-permute-start(f32[48,8,128]{2,1,0:T(8,128)S(1)} %get-tuple-element.44), channel_id=1, source_target_pairs={{0,16},{1,17},{2,18},{3,19},{4,20},{5,21},{6,22},{7,23},{8,24},{9,... | collective-permute-start | bytes 589832 | tf_op jit(solution)/shard_map/ppermute | solution.py:64
  25.0 2.1 %collective-permute-start.13 = (f32[12,8,128]{2,1,0:T(8,128)S(1)}, f32[12,8,128]{2,1,0:T(8,128)S(1)}, u32[]{:S(2)}, u32[]{:S(2)}) collective-permute-start(f32[12,8,128]{2,1,0:T(8,128)S(1)} %get-tuple-element.48), channel_id=1, source_target_pairs={{0,1},{1,0},{2,3},{3,2},{4,5},{5,4},{6,7},{7,6},{8,9},{9,8},{10,11... | collective-permute-start | bytes 147464 | tf_op jit(solution)/shard_map/ppermute | solution.py:64
  25.0 12.7 %collective-permute-start.11 = (f32[64,8,128]{2,1,0:T(8,128)S(1)}, f32[64,8,128]{2,1,0:T(8,128)S(1)}, u32[]{:S(2)}, u32[]{:S(2)}) collective-permute-start(f32[64,8,128]{2,1,0:T(8,128)S(1)} %get-tuple-element.46), channel_id=1, source_target_pairs={{0,4},{1,5},{2,6},{3,7},{4,0},{5,1},{6,2},{7,3},{8,12},{9,13},{10,... | collective-permute-start | bytes 786440 | tf_op jit(solution)/shard_map/ppermute | solution.py:64
  26.9 10.8 %collective-permute-start.12 = (f32[64,8,128]{2,1,0:T(8,128)S(1)}, f32[64,8,128]{2,1,0:T(8,128)S(1)}, u32[]{:S(2)}, u32[]{:S(2)}) collective-permute-start(f32[64,8,128]{2,1,0:T(8,128)S(1)} %get-tuple-element.47), channel_id=1, source_target_pairs={{0,1},{1,0},{2,3},{3,2},{4,8},{5,9},{6,10},{7,11},{8,4},{9,5},{10,... | collective-permute-start | bytes 786440 | tf_op jit(solution)/shard_map/ppermute | solution.py:64
  27.1 4.2 %collective-permute-start.14 = (f32[12,8,128]{2,1,0:T(8,128)S(1)}, f32[12,8,128]{2,1,0:T(8,128)S(1)}, u32[]{:S(2)}, u32[]{:S(2)}) collective-permute-start(f32[12,8,128]{2,1,0:T(8,128)S(1)} %add.7.refs_0_), channel_id=1, source_target_pairs={{0,2},{1,3},{2,0},{3,1},{4,6},{5,7},{6,4},{7,5},{8,10},{9,11},{10,... | collective-permute-start | bytes 147464 | tf_op jit(solution)/shard_map/ppermute | solution.py:64
  28.7 9.0 %collective-permute-start.10 = (f32[48,8,128]{2,1,0:T(8,128)S(1)}, f32[48,8,128]{2,1,0:T(8,128)S(1)}, u32[]{:S(2)}, u32[]{:S(2)}) collective-permute-start(f32[48,8,128]{2,1,0:T(8,128)S(1)} %get-tuple-element.45), channel_id=1, source_target_pairs={{0,16},{1,17},{2,18},{3,19},{4,20},{5,21},{6,22},{7,23},{8,24},{9,... | collective-permute-start | bytes 589832 | tf_op jit(solution)/shard_map/ppermute | solution.py:64
  31.3 4.3 %collective-permute-start.15 = (f32[12,8,128]{2,1,0:T(8,128)S(1)}, f32[12,8,128]{2,1,0:T(8,128)S(1)}, u32[]{:S(2)}, u32[]{:S(2)}) collective-permute-start(f32[12,8,128]{2,1,0:T(8,128)S(1)} %shard_map.47.refs_5_.v_here.refs_7_), channel_id=1, source_target_pairs={{0,17},{1,16},{2,19},{3,18},{4,21},{5,20},{6,23},{7,22},{8,25},{9,... | collective-permute-start | bytes 147464 | tf_op jit(solution)/shard_map/ppermute | solution.py:64
  35.6 6.4 %collective-permute-start.16 = (f32[34,8,128]{2,1,0:T(8,128)S(1)}, f32[34,8,128]{2,1,0:T(8,128)S(1)}, u32[]{:S(2)}, u32[]{:S(2)}) collective-permute-start(f32[34,8,128]{2,1,0:T(8,128)S(1)} %get-tuple-element.54), channel_id=1, source_target_pairs={{0,4},{1,5},{2,6},{3,7},{4,0},{5,1},{6,2},{7,3},{8,12},{9,13},{10,... | collective-permute-start | bytes 417800 | tf_op jit(solution)/shard_map/ppermute | solution.py:64
  37.4 4.7 %collective-permute-start.17 = (f32[34,8,128]{2,1,0:T(8,128)S(1)}, f32[34,8,128]{2,1,0:T(8,128)S(1)}, u32[]{:S(2)}, u32[]{:S(2)}) collective-permute-start(f32[34,8,128]{2,1,0:T(8,128)S(1)} %get-tuple-element.55), channel_id=1, source_target_pairs={{0,1},{1,0},{2,3},{3,2},{4,8},{5,9},{6,10},{7,11},{8,4},{9,5},{10,... | collective-permute-start | bytes 417800 | tf_op jit(solution)/shard_map/ppermute | solution.py:64
